TPU v7x, 256 devices: a whole 4x4x8 slice. The times are simulated.
256 devices in a mesh: lat: 32 (over z, y_lo, core), lon: 8 (over x, y_hi).
Axes of the slice: x: 4, y: 4 (y_hi: 2, y_lo: 2; y = y_hi * 2 + y_lo), z: 8, core: 2. Of those that a mesh axis runs over, the one named last changes fastest.
Arguments:
- eastward_speed_face: float32 [72, 1024, 1024], P(None, 'lat', 'lon'), may hold values from -6 to 6
- northward_speed_face: float32 [72, 1024, 1024], P(None, 'lat', 'lon'), may hold values from -6 to 6
- stratum_extent_east_face: float32 [72, 1024, 1024], P(None, 'lat', 'lon'), may hold values from 0.5 to 2
- stratum_extent_north_face: float32 [72, 1024, 1024], P(None, 'lat', 'lon'), may hold values from 0.5 to 2
- northward_span_east_face: float32 [1024, 1024], P('lat', 'lon'), may hold values from 0.5 to 2
- eastward_span_north_face: float32 [1024, 1024], P('lat', 'lon'), may hold values from 0.5 to 2
- ocean_flag_east_face: int32 [72, 1024, 1024], P(None, 'lat', 'lon'), may hold values 0 or 1
- ocean_flag_north_face: int32 [72, 1024, 1024], P(None, 'lat', 'lon'), may hold values 0 or 1
- counterpart_across_seam: int32 [1024], replicated, may hold values from 0 to 1023, as said below
Outputs:
- eastward_speed_next: float32 [72, 1024, 1024], P(None, 'lat', 'lon')
- northward_speed_next: float32 [72, 1024, 1024], P(None, 'lat', 'lon')
Inputs may be any that keep to these rules, and one draw needn't show every extreme that they name: counterpart_across_seam[i] = (p - 1 - i) mod 1024 for one pivot p drawn anew in each draw; it is its own inverse.
All inputs are finite; a program needn't handle non-finite values. No bound on the sum of `ocean_flag_east_face` or of `ocean_flag_north_face` on one device may be relied on, other than what follows from the above.
Results may differ from a plain program's by a relative error of at most 0.00002.
Values sent between devices are 32-bit elements; how exact they have to be, the bound alone decides.
A program may use at most 128 MiB of HBM per device.

v0:
```python
import jax
import jax.numpy as jnp
from jax import lax
from jax.sharding import PartitionSpec as P

time_step = 0.2


def extended_2(block, sides, width, periodic):
    for axis, dim in sides:
        count = lax.axis_size(axis)
        forward = [(i, i + 1) for i in range(count - 1)]
        if periodic:
            forward.append((count - 1, 0))
        backward = [(target, source) for source, target in forward]
        low = lax.ppermute(
            lax.slice_in_dim(block, block.shape[dim] - width, None, axis=dim), axis, forward
        )
        high = lax.ppermute(lax.slice_in_dim(block, 0, width, axis=dim), axis, backward)
        block = jnp.concatenate([low, block, high], axis=dim)
    return block


def copy_for_each(shard, axis):
    copies = jnp.broadcast_to(shard, (lax.axis_size(axis), *shard.shape))
    return lax.all_to_all(copies, axis, split_axis=0, concat_axis=0, tiled=True)


def in_order(parts, dim):
    parts = jnp.moveaxis(parts, 0, dim)
    lengths = parts.shape
    return parts.reshape(*lengths[:dim], lengths[dim] * lengths[dim + 1], *lengths[dim + 2 :])


def gathered_copies(shard, axis, dim):
    parts = copy_for_each(shard, axis)
    return in_order(parts, dim)


def interp(a, b, c, d):
    return (7.0 * (b + c) - (a + d)) / 12.0


def advect(umv, vmv, tuv, tvv, rows, cols):

    def cx(field, ro, co):
        return field[..., ro : ro + rows, co : co + cols + 1]

    def ry(field, ro, co):
        return field[..., ro : ro + rows + 1, co : co + cols]

    fut = (
        0.5
        * (cx(tuv, 2, 1) + cx(tuv, 2, 2))
        * interp(cx(umv, 2, 0), cx(umv, 2, 1), cx(umv, 2, 2), cx(umv, 2, 3))
    )
    vface = ry(tvv, 1, 2)
    fvf = (
        0.5
        * (vface + ry(tvv, 1, 3))
        * interp(ry(umv, 0, 2), ry(umv, 1, 2), ry(umv, 2, 2), ry(umv, 3, 2))
    )
    fuf = (
        0.5
        * (cx(tuv, 2, 1) + cx(tuv, 3, 1))
        * interp(cx(vmv, 2, 0), cx(vmv, 2, 1), cx(vmv, 2, 2), cx(vmv, 2, 3))
    )
    fvt = (
        0.5
        * (vface + ry(tvv, 2, 2))
        * interp(ry(vmv, 0, 2), ry(vmv, 1, 2), ry(vmv, 2, 2), ry(vmv, 3, 2))
    )
    trend_u = -(fut[..., 1:] - fut[..., :-1] + (fvf[..., 1:, :] - fvf[..., :-1, :]))
    trend_v = -(fuf[..., 1:] - fuf[..., :-1] + (fvt[..., 1:, :] - fvt[..., :-1, :]))
    return (trend_u, trend_v)


def place_fold(extended, ghosts):
    at_top = lax.axis_index("lat") == lax.axis_size("lat") - 1
    height = extended.shape[2]
    upper = extended[:, :, height - 2 :, :]
    top_rows = jnp.where(at_top, ghosts, upper)
    return lax.dynamic_update_slice_in_dim(extended, top_rows, height - 2, 2)


def local(
    eastward_speed_face,
    northward_speed_face,
    stratum_extent_east_face,
    stratum_extent_north_face,
    northward_span_east_face,
    eastward_span_north_face,
    ocean_flag_east_face,
    ocean_flag_north_face,
    counterpart_across_seam,
):
    umf = ocean_flag_east_face.astype(jnp.float32)
    northward_transport_rate = ocean_flag_north_face.astype(jnp.float32)
    um = umf * eastward_speed_face
    vm = northward_transport_rate * northward_speed_face
    volu = northward_span_east_face[None] * stratum_extent_east_face
    volv = eastward_span_north_face[None] * stratum_extent_north_face
    fields = jnp.stack([um, vm, volu * um, volv * vm])
    rows = um.shape[1]
    cols = um.shape[2]
    tall = extended_2(fields, (("lat", 2),), 2, False)
    band = gathered_copies(fields[:, :, -2:, :], "lon", 3)
    own_columns = lax.axis_index("lon") * cols + jnp.arange(cols, dtype=jnp.int32)
    ghosts = -jnp.take(band[:, :, ::-1, :], counterpart_across_seam[own_columns], axis=3)
    tall = place_fold(tall, ghosts)
    extended = extended_2(tall, (("lon", 3),), 2, True)
    trend_u, trend_v = advect(extended[0], extended[1], extended[2], extended[3], rows, cols)
    eastward_speed_next = umf * (um + time_step * trend_u / volu)
    northward_speed_next = northward_transport_rate * (vm + time_step * trend_v / volv)
    return (eastward_speed_next, northward_speed_next)


def solution(mesh):
    return jax.shard_map(
        local,
        mesh=mesh,
        in_specs=(
            P(None, "lat", "lon"),
            P(None, "lat", "lon"),
            P(None, "lat", "lon"),
            P(None, "lat", "lon"),
            P("lat", "lon"),
            P("lat", "lon"),
            P(None, "lat", "lon"),
            P(None, "lat", "lon"),
            P(),
        ),
        out_specs=(P(None, "lat", "lon"), P(None, "lat", "lon")),
        check_vma=False,
    )
```

profile of v0, /device:TPU:129, one launch (start us, length us, event | category | flops | bytes accessed | tf_op | source)
XLA Modules:
  0.0 143.4 jit_solution(11659458511595999450)
XLA Ops:
  0.6 0.0 copy-start
  0.6 0.0 copy-start.11
  0.7 0.9 copy.170
  1.6 0.0 copy-start.16
  1.6 0.8 copy.172
  2.4 3.1 %copy.171 = f32[72,32,128]{0,1,2:T(8,128)} copy(f32[72,32,128]{2,1,0:T(8,128)} %param.11) | data formatting | bytes 2359296 | tf_op args[2]
  5.6 0.0 copy-done.11
  5.6 0.0 copy-start.12
  5.6 2.1 %copy.173 = f32[72,32,128]{0,1,2:T(8,128)} copy(f32[72,32,128]{2,1,0:T(8,128)S(1)} %copy-done.11) | data formatting | bytes 2359296 | tf_op args[3]
  7.6 0.0 copy-done.12
  7.6 2.1 %copy.166 = s32[72,32,128]{0,1,2:T(8,128)} copy(s32[72,32,128]{2,1,0:T(8,128)S(1)} %copy-done.12) | data formatting | bytes 2359296 | tf_op args[6]
  9.8 0.0 copy-done.13
  9.8 2.1 %copy.168 = s32[72,32,128]{0,1,2:T(8,128)} copy(s32[72,32,128]{2,1,0:T(8,128)S(1)} %copy-done.13) | data formatting | bytes 2359296 | tf_op args[7]
  11.9 0.0 copy-done.14
  11.9 2.1 %copy.167 = f32[72,32,128]{0,1,2:T(8,128)} copy(f32[72,32,128]{2,1,0:T(8,128)S(1)} %copy-done.14) | data formatting | bytes 2359296 | tf_op args[0]
  14.0 0.0 copy-done.15
  14.0 2.1 %copy.169 = f32[72,32,128]{0,1,2:T(8,128)} copy(f32[72,32,128]{2,1,0:T(8,128)S(1)} %copy-done.15) | data formatting | bytes 2359296 | tf_op args[1]
  16.1 3.4 %multiply_multiply_fusion = (f32[72,32,128]{0,1,2:T(8,128)S(1)}, f32[72,32,128]{0,1,2:T(8,128)S(1)}) fusion(f32[72,32,128]{0,1,2:T(8,128)} %copy.173, f32[32,128]{0,1:T(8,128)S(1)} %copy.172, f32[72,32,128]{0,1,2:T(8,128)} %copy.169, s32[72,32,128]{0,1,2:T(8,128)} %copy.168), kind=kLoop, calls=%fused_computation.58 | loop fusion | flops 1179648 | bytes 5914624 | tf_op jit(solution)/shard_map/mul | solution.py:103
  19.5 0.0 copy-done.16
  19.5 0.1 copy-done.6
  19.5 0.6 copy-done.8
  20.2 0.6 copy-done.10
  20.8 0.8 multiply_multiply_fusion.1
  21.6 0.0 copy-start.2
  21.6 0.0 copy-start.5
  21.7 0.5 copy-done.4
  22.1 2.0 %pad_maximum_fusion.5 = (f32[4,72,2,128]{1,0,2,3:T(4,128)S(1)}, f32[4,72,2,128]{1,0,2,3:T(4,128)}) fusion(f32[1,72,32,128]{1,0,2,3:T(1,128)S(1)} %bitcast.38, f32[1,72,32,128]{1,0,2,3:T(1,128)S(1)} %bitcast.40, f32[1,72,32,128]{1,0,2,3:T(1,128)S(1)} %bitcast.34, f32[1,72,32,128]{1,0,2,3:T(1,128)S(1)} %bitcast.36), kind=kLoop, calls=%fused_computation.63 | loop fusion | flops 442368 | bytes 5308416 | tf_op jit(solution)/shard_map/slice | solution.py:17
  24.1 0.0 copy-done.2
  24.1 0.0 copy-done.5
  24.1 2.6 %collective-permute-start.1 = (f32[4,72,2,128]{1,0,2,3:T(4,128)}, f32[4,72,2,128]{1,0,2,3:T(4,128)S(1)}, u32[]{:S(2)}, u32[]{:S(2)}) collective-permute-start(f32[4,72,2,128]{1,0,2,3:T(4,128)} %get-tuple-element.25), channel_id=1, source_target_pairs={{8,0},{16,8},{24,16},{32,24},{40,32},{48,40},{56,48},{64,56},{72,6... | collective-permute-start | bytes 884744 | tf_op jit(solution)/shard_map/ppermute | solution.py:19
  26.7 3.1 %collective-permute-start = (f32[4,72,2,128]{1,0,2,3:T(4,128)S(1)}, f32[4,72,2,128]{1,0,2,3:T(4,128)}, u32[]{:S(2)}, u32[]{:S(2)}) collective-permute-start(f32[4,72,2,128]{1,0,2,3:T(4,128)S(1)} %get-tuple-element.24), channel_id=1, source_target_pairs={{0,8},{8,16},{16,24},{24,32},{32,40},{40,48},{48,56},{56,64},{64,7... | collective-permute-start | bytes 884744 | tf_op jit(solution)/shard_map/ppermute | solution.py:16
  29.8 0.2 copy.177
  30.0 1.7 %broadcast_in_dim.17 = f32[8,4,72,2,128]{4,2,3,1,0:T(8,128)} broadcast(f32[4,72,2,128]{3,1,2,0:T(8,128)S(1)} %copy.177), dimensions={1,2,3,4} | broadcast | bytes 2654208 | tf_op jit(solution)/shard_map/broadcast_in_dim | solution.py:25
  31.7 6.5 %all-to-all-start = ((f32[8,4,72,2,128]{4,2,3,1,0:T(8,128)}), f32[8,4,72,2,128]{4,2,3,1,0:T(8,128)}, u32[]{:S(2)}, u32[]{:S(2)}) async-start(f32[8,4,72,2,128]{4,2,3,1,0:T(8,128)} %broadcast_in_dim.17), calls=%async_computation | async-start | bytes 4718592 | tf_op jit(solution)/shard_map/all_to_all | solution.py:26
  38.3 0.0 copy-done
  38.3 1.0 gather_fusion
  39.3 1.3 collective-permute-done.1
  40.6 14.7 %collective-permute-done = f32[4,72,2,128]{1,0,2,3:T(4,128)} collective-permute-done((f32[4,72,2,128]{1,0,2,3:T(4,128)S(1)}, f32[4,72,2,128]{1,0,2,3:T(4,128)}, u32[]{:S(2)}, u32[]{:S(2)}) %collective-permute-start) | collective-permute-done | bytes 294944 | tf_op jit(solution)/shard_map/ppermute | solution.py:16
  55.3 12.8 %pad_maximum_fusion.1 = f32[4,72,36,128]{1,0,2,3:T(4,128)} fusion(f32[4,72,2,128]{1,0,2,3:T(4,128)S(1)} %collective-permute-done.1, f32[1,72,32,128]{1,0,2,3:T(1,128)} %bitcast.39, f32[1,72,32,128]{1,0,2,3:T(1,128)} %bitcast.41, f32[1,72,32,128]{1,0,2,3:T(1,128)S(1)} %bitcast.35, f32[1,72,32,128]{1,0,2,3:T(1,128)} %bitcast.37, ...), kind=kLoop, calls=%fused_computation.3 | loop fusion | flops 6635520 | bytes 10616832 | tf_op jit(solution)/shard_map/concatenate | solution.py:20
  68.0 5.5 %all-to-all-done = f32[8,4,72,2,128]{4,2,3,1,0:T(8,128)} async-done(((f32[8,4,72,2,128]{4,2,3,1,0:T(8,128)}), f32[8,4,72,2,128]{4,2,3,1,0:T(8,128)}, u32[]{:S(2)}, u32[]{:S(2)}) %all-to-all-start) | async-done | bytes 2359328 | tf_op jit(solution)/shard_map/all_to_all | solution.py:26
  73.6 4.8 %copy.208 = f32[4,72,2,8,128]{1,0,4,3,2:T(4,128)} copy(f32[4,72,2,8,128]{4,1,2,0,3:T(8,128)} %bitcast.8) | data formatting | bytes 4718592 | tf_op jit(solution)/shard_map/reshape | solution.py:32
  78.4 4.5 %rev.3 = f32[4,72,2,1024]{1,0,3,2:T(4,128)} reverse(f32[4,72,2,1024]{1,0,3,2:T(4,128)} %bitcast.42), dimensions={2} | reverse | bytes 4718592 | tf_op jit(solution)/shard_map/rev | solution.py:109
  82.9 3.1 %gather_fusion.1 = f32[128,4,72,2]{2,1,3,0:T(4,128)S(1)} fusion(f32[4,72,2,1024]{1,0,3,2:T(4,128)} %rev.3, s32[1024]{0:T(1024)S(1)} %pad_clamp_fusion), kind=kCustom, calls=%fused_computation.1 | custom fusion | bytes 590336 | tf_op jit(solution)/shard_map/jit(_take)/gather | solution.py:109
  86.0 1.1 fusion.32
  87.2 1.0 fusion.36
  88.2 3.1 %collective-permute-start.2 = (f32[4,72,36,2]{1,0,2,3:T(4,128)S(1)}, f32[4,72,36,2]{1,0,2,3:T(4,128)S(1)}, u32[]{:S(2)}, u32[]{:S(2)}) collective-permute-start(f32[4,72,36,2]{1,0,2,3:T(4,128)S(1)} %get-tuple-element.22), channel_id=1, source_target_pairs={{0,1},{1,2},{2,3},{3,4},{4,5},{5,6},{6,7},{7,0},{8,9},{9,10},{10,1... | collective-permute-start | bytes 248840 | tf_op jit(solution)/shard_map/ppermute | solution.py:16
  91.3 2.0 %collective-permute-start.3 = (f32[4,72,36,2]{1,0,2,3:T(4,128)S(1)}, f32[4,72,36,2]{1,0,2,3:T(4,128)S(1)}, u32[]{:S(2)}, u32[]{:S(2)}) collective-permute-start(f32[4,72,36,2]{1,0,2,3:T(4,128)S(1)} %get-tuple-element.23), channel_id=1, source_target_pairs={{1,0},{2,1},{3,2},{4,3},{5,4},{6,5},{7,6},{0,7},{9,8},{10,9},{11,1... | collective-permute-start | bytes 248840 | tf_op jit(solution)/shard_map/ppermute | solution.py:19
  93.3 3.8 %collective-permute-done.2 = f32[4,72,36,2]{1,0,2,3:T(4,128)S(1)} collective-permute-done((f32[4,72,36,2]{1,0,2,3:T(4,128)S(1)}, f32[4,72,36,2]{1,0,2,3:T(4,128)S(1)}, u32[]{:S(2)}, u32[]{:S(2)}) %collective-permute-start.2) | collective-permute-done | bytes 82976 | tf_op jit(solution)/shard_map/ppermute | solution.py:16
  97.1 3.7 %collective-permute-done.3 = f32[4,72,36,2]{1,0,2,3:T(4,128)S(1)} collective-permute-done((f32[4,72,36,2]{1,0,2,3:T(4,128)S(1)}, f32[4,72,36,2]{1,0,2,3:T(4,128)S(1)}, u32[]{:S(2)}, u32[]{:S(2)}) %collective-permute-start.3) | collective-permute-done | bytes 82976 | tf_op jit(solution)/shard_map/ppermute | solution.py:19
  100.8 10.1 %pad_maximum_fusion = f32[4,72,36,132]{1,0,2,3:T(4,128)S(1)} fusion(f32[4,72,36,2]{1,0,2,3:T(4,128)S(1)} %collective-permute-done.3, f32[4,72,36,128]{1,0,2,3:T(4,128)} %fusion.32, f32[4,72,36,2]{1,0,2,3:T(4,128)S(1)} %collective-permute-done.2), kind=kLoop, calls=%fused_computation.2 | loop fusion | flops 2737152 | bytes 10948608 | tf_op jit(solution)/shard_map/concatenate | solution.py:20
  110.9 7.2 %fusion.35 = (f32[1,72,36,132]{1,0,2,3:T(1,128)S(1)}, f32[1,72,36,132]{1,0,2,3:T(1,128)S(1)}, f32[1,72,36,132]{1,0,2,3:T(1,128)S(1)}, f32[1,72,36,132]{1,0,2,3:T(1,128)S(1)}) fusion(f32[4,72,36,132]{1,0,2,3:T(4,128)S(1)} %pad_maximum_fusion), kind=kLoop, calls=%fused_computation.74 | loop fusion | bytes 10948608 | tf_op jit(solution)/shard_map/slice | solution.py:112
  118.0 0.4 copy_bitcast_fusion
  118.4 0.4 copy_bitcast_fusion.2
  118.7 4.7 %fusion.12 = (f32[72,32,129]{0,1,2:T(8,128)}, f32[72,32,129]{0,1,2:T(8,128)S(1)}) fusion(f32[72,36,132]{0,1,2:T(8,128)S(1)} %get-tuple-element.30, f32[72,36,132]{0,1,2:T(8,128)S(1)} %get-tuple-element.33, f32[72,36,132]{0,1,2:T(8,128)S(1)} %get-tuple-element.32), kind=kLoop, calls=%fused_computation.27 | loop fusion | flops 4755456 | bytes 15455232 | tf_op jit(solution)/shard_map/mul | solution.py:64
  123.4 4.1 %fusion.2 = (f32[72,33,128]{0,1,2:T(8,128)}, f32[72,33,128]{0,1,2:T(8,128)S(1)}) fusion(f32[72,36,132]{0,1,2:T(8,128)S(1)} %get-tuple-element.30, f32[72,36,132]{0,1,2:T(8,128)S(1)} %get-tuple-element.31, f32[72,36,132]{0,1,2:T(8,128)S(1)} %get-tuple-element.32), kind=kLoop, calls=%fused_computation.11 | loop fusion | flops 4866048 | bytes 15814656 | tf_op jit(solution)/shard_map/mul | solution.py:69
  127.5 0.0 copy-done.3
  127.5 0.0 copy-done.7
  127.6 0.0 copy-done.9
  127.6 0.0 copy-done.17
  127.6 2.6 %fusion.31 = f32[72,32,128]{0,1,2:T(8,128)} fusion(f32[72,32,128]{0,1,2:T(8,128)S(1)} %copy-done.3, f32[72,33,128]{0,1,2:T(8,128)S(1)} %get-tuple-element.29, f32[72,32,129]{0,1,2:T(8,128)S(1)} %get-tuple-element.27, s32[72,32,128]{0,1,2:T(8,128)S(1)} %copy-done.9, f32[72,32,128]{0,1,2:T(8,128)S(1)} %copy-done.7, f32[32,128]{0,1:T(8,128)S(1)} %copy-done.17), kind=kLoop, calls=%fused_computation.54 | loop fusion | flops 2949120 | bytes 9453568 | tf_op jit(solution)/shard_map/mul | solution.py:113
  130.2 3.1 %copy.206 = f32[72,32,128]{2,1,0:T(8,128)} copy(f32[72,32,128]{0,1,2:T(8,128)} %fusion.31) | data formatting | bytes 2359296
  133.3 7.0 %fusion.25 = f32[72,32,128]{0,1,2:T(8,128)} fusion(f32[72,32,128]{0,1,2:T(8,128)S(1)} %get-tuple-element.17, f32[72,33,128]{0,1,2:T(8,128)} %get-tuple-element.28, f32[72,32,129]{0,1,2:T(8,128)} %get-tuple-element.26, s32[72,32,128]{0,1,2:T(8,128)} %copy.168, f32[72,32,128]{0,1,2:T(8,128)} %copy.173, f32[32,128]{0,1:T(8,128)S(1)} %copy.172), kind=kLoop, calls=%fused_computation.46 | loop fusion | flops 2949120 | bytes 9453568 | tf_op jit(solution)/shard_map/mul | solution.py:114
  140.3 3.1 %copy.207 = f32[72,32,128]{2,1,0:T(8,128)} copy(f32[72,32,128]{0,1,2:T(8,128)} %fusion.25) | data formatting | bytes 2359296
  143.4 0.0 copy-done.1
  (17 shorter events, 0.0 us)
Async XLA Ops:
  0.6 37.6 %copy-start = (s32[1024]{0:T(1024)S(1)}, s32[1024]{0:T(1024)}, u32[]{:S(2)}) copy-start(s32[1024]{0:T(1024)} %param.17) | copy-start | bytes 12292
  0.6 4.9 %copy-start.11 = (f32[72,32,128]{2,1,0:T(8,128)S(1)}, f32[72,32,128]{2,1,0:T(8,128)}, u32[]{:S(2)}) copy-start(f32[72,32,128]{2,1,0:T(8,128)} %param.12) | copy-start | bytes 3538948
  1.6 17.9 %copy-start.16 = (f32[32,128]{0,1:T(8,128)}, f32[32,128]{0,1:T(8,128)S(1)}, u32[]{:S(2)}) copy-start(f32[32,128]{0,1:T(8,128)S(1)} %copy.170) | copy-start | bytes 49156
  5.6 2.1 %copy-start.12 = (s32[72,32,128]{2,1,0:T(8,128)S(1)}, s32[72,32,128]{2,1,0:T(8,128)}, u32[]{:S(2)}) copy-start(s32[72,32,128]{2,1,0:T(8,128)} %param.15) | copy-start | bytes 3538948
  7.6 2.2 %copy-start.13 = (s32[72,32,128]{2,1,0:T(8,128)S(1)}, s32[72,32,128]{2,1,0:T(8,128)}, u32[]{:S(2)}) copy-start(s32[72,32,128]{2,1,0:T(8,128)} %param.16) | copy-start | bytes 3538948
  9.8 2.2 %copy-start.14 = (f32[72,32,128]{2,1,0:T(8,128)S(1)}, f32[72,32,128]{2,1,0:T(8,128)}, u32[]{:S(2)}) copy-start(f32[72,32,128]{2,1,0:T(8,128)} %param.9) | copy-start | bytes 3538948
  11.9 2.1 %copy-start.15 = (f32[72,32,128]{2,1,0:T(8,128)S(1)}, f32[72,32,128]{2,1,0:T(8,128)}, u32[]{:S(2)}) copy-start(f32[72,32,128]{2,1,0:T(8,128)} %param.10) | copy-start | bytes 3538948
  16.1 3.5 %copy-start.6 = (f32[72,32,128]{0,1,2:T(8,128)S(1)}, f32[72,32,128]{0,1,2:T(8,128)}, u32[]{:S(2)}) copy-start(f32[72,32,128]{0,1,2:T(8,128)} %copy.171) | copy-start | bytes 3538948
  16.1 4.1 %copy-start.8 = (s32[72,32,128]{0,1,2:T(8,128)S(1)}, s32[72,32,128]{0,1,2:T(8,128)}, u32[]{:S(2)}) copy-start(s32[72,32,128]{0,1,2:T(8,128)} %copy.166) | copy-start | bytes 3538948
  16.1 4.7 %copy-start.10 = (f32[72,32,128]{0,1,2:T(8,128)S(1)}, f32[72,32,128]{0,1,2:T(8,128)}, u32[]{:S(2)}) copy-start(f32[72,32,128]{0,1,2:T(8,128)} %copy.167) | copy-start | bytes 3538948
  20.8 1.3 copy-start.4
  21.6 2.5 %copy-start.2 = (f32[72,32,128]{0,1,2:T(8,128)}, f32[72,32,128]{0,1,2:T(8,128)S(1)}, u32[]{:S(2)}) copy-start(f32[72,32,128]{0,1,2:T(8,128)S(1)} %get-tuple-element.15) | copy-start | bytes 3538948
  21.6 2.5 %copy-start.5 = (f32[72,32,128]{0,1,2:T(8,128)}, f32[72,32,128]{0,1,2:T(8,128)S(1)}, u32[]{:S(2)}) copy-start(f32[72,32,128]{0,1,2:T(8,128)S(1)} %get-tuple-element.14) | copy-start | bytes 3538948
  24.1 16.4 %collective-permute-start.1 = (f32[4,72,2,128]{1,0,2,3:T(4,128)}, f32[4,72,2,128]{1,0,2,3:T(4,128)S(1)}, u32[]{:S(2)}, u32[]{:S(2)}) collective-permute-start(f32[4,72,2,128]{1,0,2,3:T(4,128)} %get-tuple-element.25), channel_id=1, source_target_pairs={{8,0},{16,8},{24,16},{32,24},{40,32},{48,40},{56,48},{64,56},{72,6... | collective-permute-start | bytes 884744 | tf_op jit(solution)/shard_map/ppermute | solution.py:19
  26.7 28.5 %collective-permute-start = (f32[4,72,2,128]{1,0,2,3:T(4,128)S(1)}, f32[4,72,2,128]{1,0,2,3:T(4,128)}, u32[]{:S(2)}, u32[]{:S(2)}) collective-permute-start(f32[4,72,2,128]{1,0,2,3:T(4,128)S(1)} %get-tuple-element.24), channel_id=1, source_target_pairs={{0,8},{8,16},{16,24},{24,32},{32,40},{40,48},{48,56},{56,64},{64,7... | collective-permute-start | bytes 884744 | tf_op jit(solution)/shard_map/ppermute | solution.py:16
  31.7 41.8 %all-to-all-start = ((f32[8,4,72,2,128]{4,2,3,1,0:T(8,128)}), f32[8,4,72,2,128]{4,2,3,1,0:T(8,128)}, u32[]{:S(2)}, u32[]{:S(2)}) async-start(f32[8,4,72,2,128]{4,2,3,1,0:T(8,128)} %broadcast_in_dim.17), calls=%async_computation | async-start | bytes 4718592 | tf_op jit(solution)/shard_map/all_to_all | solution.py:26
  88.2 8.9 %collective-permute-start.2 = (f32[4,72,36,2]{1,0,2,3:T(4,128)S(1)}, f32[4,72,36,2]{1,0,2,3:T(4,128)S(1)}, u32[]{:S(2)}, u32[]{:S(2)}) collective-permute-start(f32[4,72,36,2]{1,0,2,3:T(4,128)S(1)} %get-tuple-element.22), channel_id=1, source_target_pairs={{0,1},{1,2},{2,3},{3,4},{4,5},{5,6},{6,7},{7,0},{8,9},{9,10},{10,1... | collective-permute-start | bytes 248840 | tf_op jit(solution)/shard_map/ppermute | solution.py:16
  91.3 9.5 %collective-permute-start.3 = (f32[4,72,36,2]{1,0,2,3:T(4,128)S(1)}, f32[4,72,36,2]{1,0,2,3:T(4,128)S(1)}, u32[]{:S(2)}, u32[]{:S(2)}) collective-permute-start(f32[4,72,36,2]{1,0,2,3:T(4,128)S(1)} %get-tuple-element.23), channel_id=1, source_target_pairs={{1,0},{2,1},{3,2},{4,3},{5,4},{6,5},{7,6},{0,7},{9,8},{10,9},{11,1... | collective-permute-start | bytes 248840 | tf_op jit(solution)/shard_map/ppermute | solution.py:19
  123.4 4.1 %copy-start.3 = (f32[72,32,128]{0,1,2:T(8,128)S(1)}, f32[72,32,128]{0,1,2:T(8,128)}, u32[]{:S(2)}) copy-start(f32[72,32,128]{0,1,2:T(8,128)} %copy-done.2) | copy-start | bytes 3538948
  123.4 4.1 %copy-start.7 = (f32[72,32,128]{0,1,2:T(8,128)S(1)}, f32[72,32,128]{0,1,2:T(8,128)}, u32[]{:S(2)}) copy-start(f32[72,32,128]{0,1,2:T(8,128)} %copy.171) | copy-start | bytes 3538948
  123.4 4.1 %copy-start.9 = (s32[72,32,128]{0,1,2:T(8,128)S(1)}, s32[72,32,128]{0,1,2:T(8,128)}, u32[]{:S(2)}) copy-start(s32[72,32,128]{0,1,2:T(8,128)} %copy.166) | copy-start | bytes 3538948
  123.4 4.1 %copy-start.17 = (f32[32,128]{0,1:T(8,128)S(1)}, f32[32,128]{0,1:T(8,128)}, u32[]{:S(2)}) copy-start(f32[32,128]{0,1:T(8,128)} %copy-done.16) | copy-start | bytes 49156
  133.3 10.1 %copy-start.1 = (s32[1024]{0:T(1024)S(1)}, s32[1024]{0:T(1024)}, u32[]{:S(2)}) copy-start(s32[1024]{0:T(1024)} %param.17) | copy-start | bytes 12292
where the time goes:
time: 144 us; the launch traced here: 143 us
  other arithmetic  48.6 us (34%)
  local copies, waits for them, and re-layouts  47.6 us (33%)
  waiting for transfers between devices  28.9 us (20%)
  starting transfers between devices  17.4 us (12%)
    unnamed x46, local copies, waits for them, and re-layouts  23.4 us
    concatenate x2, other arithmetic, extended_2(): block = jnp.concatenate([low, block, high], axis=dim)  22.9 us
    ppermute x2, waiting for transfers between devices, extended_2(): lax.ppermute(lax.slice_in_dim(block, block.shape[dim] - width, None, axis...  18.4 us
    slice x1, local copies, waits for them, and re-layouts, local(): extended[1]  7.15 us
    mul x1, other arithmetic, local(): northward_transport_rate * (vm + time_step * trend_v / volv)  7.02 us
    all_to_all x1, starting transfers between devices, copy_for_each(): return lax.all_to_all(copies, axis, split_axis=0, concat_axis=0, tiled=True)  6.53 us
    ppermute x2, starting transfers between devices, extended_2(): lax.ppermute(lax.slice_in_dim(block, block.shape[dim] - width, None, axis...  6.24 us
    all_to_all x1, waiting for transfers between devices, copy_for_each(): return lax.all_to_all(copies, axis, split_axis=0, concat_axis=0, tiled=True)  5.52 us
  transfers between devices with their start and end apart: 5, of which 5 were waited for; matrix products, arithmetic and copies ran while one was open for 11% of the time, Pallas kernels for 0%

commit v1 on v0

v1 whole, which is shorter than its diff:
```python
import functools

import jax
import jax.numpy as jnp
from jax import lax
from jax.experimental import pallas as pl
from jax.experimental.pallas import tpu as pltpu
from jax.sharding import PartitionSpec as P

MESH = pl.DeviceIdType.MESH
f32 = jnp.float32

FACTOR = 0.2 * 0.5 / 12.0
PAD = 8


def local_copy(src, dst, sem):
    return pltpu.make_async_copy(src, dst, sem)


def kernel(n_lat, n_lon, L, R, C, u, v, eu, ev, wu, wv, mu, mv, seam, ou, ov, *scratch):
    (
        us, vs, eus, evs, wus, wvs, mus, mvs, seams,
        pu, pv, pmu, pmv, peu, pev,
        UM, VM, TU, TV, H,
        SN, SS, SF, EB, WB, CN, CS,
        RS, RN, RW, RE, RCS, RCN, G,
        in_sem, row_sem, send_sem, recv_sem, fold_send, fold_recv,
    ) = scratch
    lat = lax.axis_index("lat")
    lon = lax.axis_index("lon")
    east = lax.rem(lon + 1, n_lon)
    west = lax.rem(lon + n_lon - 1, n_lon)
    has_north = lat < n_lat - 1
    has_south = lat > 0
    pitch = R + 2 * PAD
    blocks = L // 4

    rows = (0, 1, R - 2, R - 1)
    loads = []
    for src, dst in ((u, pu), (v, pv), (mu, pmu), (mv, pmv)):
        for i, r in enumerate(rows):
            loads.append((src.at[:, r, :], dst.at[i]))
    for src, dst in ((eu, peu), (ev, pev)):
        for i, r in enumerate((0, R - 1)):
            loads.append((src.at[:, r, :], dst.at[i]))
    loads.append((wu, wus))
    loads.append((wv, wvs))
    loads.append((seam, seams))
    row_copies = [local_copy(s, d, row_sem.at[i]) for i, (s, d) in enumerate(loads)]
    full_copies = [
        local_copy(s, d, in_sem.at[i])
        for i, (s, d) in enumerate(((u, us), (mu, mus), (v, vs), (mv, mvs), (eu, eus), (ev, evs)))
    ]
    for copy in row_copies:
        copy.start()
    for copy in full_copies:
        copy.start()

    barrier = pltpu.get_barrier_semaphore()

    def greet(a, b):
        pl.semaphore_signal(barrier, inc=1, device_id={"lat": a, "lon": b}, device_id_type=MESH)

    greet(lat, east)
    greet(lat, west)

    @pl.when(has_north)
    def _():
        greet(lat + 1, lon)
        greet(lat + 1, west)

    @pl.when(has_south)
    def _():
        greet(lat - 1, lon)
        greet(lat - 1, east)

    @pl.when(jnp.logical_not(has_north))
    def _():
        for k in range(2, n_lon - 1):
            greet(lat, lax.rem(lon + k, n_lon))

    for copy in row_copies:
        copy.wait()

    lane = lax.broadcasted_iota(jnp.int32, (L, C), 1)
    um0 = pmu[0].astype(f32) * pu[0]
    um1 = pmu[1].astype(f32) * pu[1]
    vm0 = pmv[0].astype(f32) * pv[0]
    vm1 = pmv[1].astype(f32) * pv[1]
    SS[0] = um0
    SS[1] = um1
    SS[2] = vm0
    SS[3] = vm1
    SS[4] = wus[0:1, :] * peu[0] * um0
    SS[5] = wvs[0:1, :] * pev[0] * vm0
    um30 = pmu[2].astype(f32) * pu[2]
    um31 = pmu[3].astype(f32) * pu[3]
    vm30 = pmv[2].astype(f32) * pv[2]
    vm31 = pmv[3].astype(f32) * pv[3]
    tu31 = wus[R - 1 : R, :] * peu[1] * um31
    tv31 = wvs[R - 1 : R, :] * pev[1] * vm31
    SN[0] = um30
    SN[1] = um31
    SN[2] = vm30
    SN[3] = vm31
    SN[4] = tv31
    fill = jnp.zeros((C - L, C), f32)
    CN[...] = jnp.concatenate([tv31, fill], axis=0).T[0:8, :]
    CS[...] = jnp.concatenate([SS[4], fill], axis=0).T[C - 8 : C, :]

    pivot = seams[0] + 1
    tile = pivot // C
    turn = lax.rem(pivot, C)

    @pl.when(jnp.logical_not(has_north))
    def _():
        index = (turn + (2 * C - 1) - lane) & (C - 1)
        for i, plane in enumerate((um31, um30, vm31, vm30, tu31, tv31)):
            SF[i] = -jnp.take_along_axis(plane, index, axis=1)

    @pl.when(has_north & has_south)
    def _():
        pl.semaphore_wait(barrier, 6)

    @pl.when(jnp.logical_not(has_south))
    def _():
        pl.semaphore_wait(barrier, 4)

    @pl.when(jnp.logical_not(has_north))
    def _():
        pl.semaphore_wait(barrier, n_lon + 1)

    def send(src, dst, i, a, b):
        return pltpu.make_async_remote_copy(
            src_ref=src, dst_ref=dst, send_sem=send_sem.at[i], recv_sem=recv_sem.at[i],
            device_id={"lat": a, "lon": b}, device_id_type=MESH,
        )

    to_north = send(SN, RS, 0, lat + 1, lon)
    to_south = send(SS, RN, 1, lat - 1, lon)
    to_east = send(EB, RW, 2, lat, east)
    to_west = send(WB, RE, 3, lat, west)
    to_northwest = send(CN, RCS, 4, lat + 1, west)
    to_southeast = send(CS, RCN, 5, lat - 1, east)

    def fold_copy(k, slot):
        return pltpu.make_async_remote_copy(
            src_ref=SF, dst_ref=G.at[slot], send_sem=fold_send.at[k], recv_sem=fold_recv.at[slot],
            device_id={"lat": lat, "lon": lax.rem(lon + k, n_lon)}, device_id_type=MESH,
        )

    @pl.when(has_north)
    def _():
        to_north.start()
        to_northwest.start()

    @pl.when(has_south)
    def _():
        to_south.start()
        to_southeast.start()

    @pl.when(jnp.logical_not(has_north))
    def _():
        for k in range(1, n_lon):
            fold_copy(k, lon).start()

    for copy in full_copies:
        copy.wait()
    lanes = lax.broadcasted_iota(jnp.int32, (4 * R, C), 1)
    wide_u = jnp.concatenate([wus[...]] * 4, axis=0)
    wide_v = jnp.concatenate([wvs[...]] * 4, axis=0)

    def pack(g, carry):
        def whole(ref):
            return ref[pl.ds(g * 4, 4)].reshape(4 * R, C)

        um = whole(mus).astype(f32) * whole(us)
        vm = whole(mvs).astype(f32) * whole(vs)
        tu = wide_u * whole(eus) * um
        tv = wide_v * whole(evs) * vm
        for i in range(4):
            to = pl.ds(pl.multiple_of((g * 4 + i) * pitch + PAD, 8), R)
            UM[to, :] = um[i * R : (i + 1) * R]
            VM[to, :] = vm[i * R : (i + 1) * R]
            TU[to, :] = tu[i * R : (i + 1) * R]
            TV[to, :] = tv[i * R : (i + 1) * R]
        both = jnp.where((lanes >= 2) & (lanes <= 5), pltpu.roll(vm, 4, 1), um)
        both = jnp.where((lanes == 6) | (lanes == 7), pltpu.roll(tu, 7, 1), both)
        both = jnp.where(lanes == C - 3, pltpu.roll(tv, C - 3, 1), both)
        turned = both.T
        for f, r in enumerate((C - 2, C - 1, 2, 3, 6)):
            EB[f, pl.ds(g, 1), :] = turned[r : r + 1, :]
        for f, r in enumerate((0, 1, 4, 5, 7, C - 3)):
            WB[f, pl.ds(g, 1), :] = turned[r : r + 1, :]
        return carry

    lax.fori_loop(0, blocks, pack, 0)
    to_east.start()
    to_west.start()

    to_east.wait_recv()
    to_west.wait_recv()
    sub = lax.broadcasted_iota(jnp.int32, (8, C), 0)

    def stacked(parts):
        out = jnp.zeros((8, C), f32)
        for r, row in parts:
            out = jnp.where(sub == r, jnp.broadcast_to(row, (8, C)), out)
        return out

    def unpack(g, carry):
        w = [RW[f, pl.ds(g, 1), :] for f in range(5)]
        e = [RE[f, pl.ds(g, 1), :] for f in range(6)]
        first = stacked(list(enumerate((e[0], e[1], w[2], w[3], e[2], e[3], w[4], e[4]))))
        last = stacked(((5, e[5]), (6, w[0]), (7, w[1])))
        turned = jnp.concatenate([first, jnp.zeros((C - 16, C), f32), last], axis=0).T
        for i in range(4):
            to = pl.ds(pl.multiple_of((g * 4 + i) * pitch + PAD, 8), R)
            H[to, :] = turned[i * R : (i + 1) * R]
        return carry

    lax.fori_loop(0, blocks, unpack, 0)

    def row_of(r):
        return pl.ds(PAD + r, L, stride=pitch)

    @pl.when(has_south)
    def _():
        to_north.wait_recv()
        to_northwest.wait_recv()
        UM[row_of(-2), :] = RS[0]
        UM[row_of(-1), :] = RS[1]
        VM[row_of(-2), :] = RS[2]
        VM[row_of(-1), :] = RS[3]
        TV[row_of(-1), :] = RS[4]
        last = stacked(((5, RCS[0:1, :]),))
        H[row_of(-1), :] = jnp.concatenate([jnp.zeros((C - 8, C), f32), last], axis=0).T[0:L, :]

    @pl.when(jnp.logical_not(has_south))
    def _():
        zero = jnp.zeros((L, C), f32)
        UM[row_of(-2), :] = zero
        UM[row_of(-1), :] = zero
        VM[row_of(-2), :] = zero
        VM[row_of(-1), :] = zero
        TV[row_of(-1), :] = zero
        H[row_of(-1), :] = zero

    north = ((UM, 0), (UM, 1), (VM, 0), (VM, 1), (TU, 0), (TV, 0))

    @pl.when(has_north)
    def _():
        to_south.wait_recv()
        to_southeast.wait_recv()
        for i, (field, r) in enumerate(north):
            field[row_of(R + r), :] = RN[i]
        first = stacked(((6, RCN[7:8, :]),))
        H[row_of(R), :] = jnp.concatenate([first, jnp.zeros((C - 8, C), f32)], axis=0).T[0:L, :]

    @pl.when(jnp.logical_not(has_north))
    def _():
        for k in range(1, n_lon):
            fold_copy(k, lax.rem(lon + n_lon - k, n_lon)).wait_recv()
        G[lon] = SF[...]
        low = lax.rem(tile - lon + 2 * n_lon, n_lon)
        high = lax.rem(tile - lon + 2 * n_lon - 1, n_lon)
        for i, (field, r) in enumerate(north):
            field[row_of(R + r), :] = jnp.where(lane < turn, G[low, i], G[high, i])
        H[row_of(R), :] = pltpu.roll(G[low, 4], 7, 1)

    col = lax.broadcasted_iota(jnp.int32, (8, C), 1)

    def left1(x, h):
        return pltpu.roll(jnp.where(col == C - 1, h, x), 1, 1)

    def left2(x, h):
        return pltpu.roll(jnp.where(col >= C - 2, h, x), 2, 1)

    def right1(x, h):
        return pltpu.roll(jnp.where(col == 0, h, x), C - 1, 1)

    def right2(x, h):
        return pltpu.roll(jnp.where(col <= 1, h, x), C - 2, 1)

    def q(a, b, c, d):
        return 7.0 * (b + c) - (a + d)

    def level(k, carry):
        for b in range(R // 8):
            base = pl.multiple_of(k * pitch + PAD + 8 * b, 8)
            at = pl.ds(8 * b, 8)

            def get(ref, o):
                return ref[pl.ds(base + o, 8), :]

            h0, hp, hm = get(H, 0), get(H, 1), get(H, -1)
            um2, um1, u0, up1, up2 = (get(UM, o) for o in (-2, -1, 0, 1, 2))
            vm2, vm1, v0, vp1, vp2 = (get(VM, o) for o in (-2, -1, 0, 1, 2))
            t0, t1 = get(TU, 0), get(TU, 1)
            sm, s0, sp = get(TV, -1), get(TV, 0), get(TV, 1)
            volu = wus[8 * b : 8 * b + 8, :] * eus[k, at, :]
            volv = wvs[8 * b : 8 * b + 8, :] * evs[k, at, :]

            a1, a2, b1, b2 = left1(u0, h0), left2(u0, h0), right1(u0, h0), right2(u0, h0)
            ht = pltpu.roll(h0, C - 7, 1)
            htp = pltpu.roll(hp, C - 7, 1)
            tl, tr = left1(t0, ht), right1(t0, ht)
            du = (t0 + tr) * q(a1, u0, b1, b2) - (tl + t0) * q(a2, a1, u0, b1)
            sr = right1(s0, pltpu.roll(h0, 3, 1))
            smr = right1(sm, pltpu.roll(hm, 3, 1))
            du = du + ((s0 + sr) * q(um1, u0, up1, up2) - (sm + smr) * q(um2, um1, u0, up1))
            ou[k, at, :] = mus[k, at, :].astype(f32) * (u0 - FACTOR * du / volu)

            hv = pltpu.roll(h0, C - 4, 1)
            c1, c2, d1, d2 = left1(v0, hv), left2(v0, hv), right1(v0, hv), right2(v0, hv)
            ts = t0 + t1
            tsl = left1(ts, ht + htp)
            dv = ts * q(c1, v0, d1, d2) - tsl * q(c2, c1, v0, d1)
            dv = dv + ((s0 + sp) * q(vm1, v0, vp1, vp2) - (sm + s0) * q(vm2, vm1, v0, vp1))
            ov[k, at, :] = mvs[k, at, :].astype(f32) * (v0 - FACTOR * dv / volv)
        return carry

    lax.fori_loop(0, L, level, 0)

    to_east.wait_send()
    to_west.wait_send()

    @pl.when(has_north)
    def _():
        to_north.wait_send()
        to_northwest.wait_send()

    @pl.when(has_south)
    def _():
        to_south.wait_send()
        to_southeast.wait_send()

    @pl.when(jnp.logical_not(has_north))
    def _():
        for k in range(1, n_lon):
            fold_copy(k, lon).wait_send()


def local(n_lat, n_lon, u, v, eu, ev, wu, wv, mu, mv, seam):
    L, R, C = u.shape
    cube = (L, R, C)
    pitch = R + 2 * PAD
    vm = pltpu.VMEM
    scratch = (
        [vm(cube, f32)] * 4
        + [vm((R, C), f32)] * 2
        + [vm(cube, jnp.int32)] * 2
        + [pltpu.SMEM(seam.shape, jnp.int32)]
        + [vm((4, L, C), f32)] * 2
        + [vm((4, L, C), jnp.int32)] * 2
        + [vm((2, L, C), f32)] * 2
        + [vm((L * pitch, C), f32)] * 5
        + [vm((5, L, C), f32), vm((6, L, C), f32), vm((6, L, C), f32)]
        + [vm((5, L // 4, C), f32), vm((6, L // 4, C), f32)]
        + [vm((8, C), f32)] * 2
        + [vm((5, L, C), f32), vm((6, L, C), f32)]
        + [vm((5, L // 4, C), f32), vm((6, L // 4, C), f32)]
        + [vm((8, C), f32)] * 2
        + [vm((n_lon, 6, L, C), f32)]
        + [
            pltpu.SemaphoreType.DMA((6,)),
            pltpu.SemaphoreType.DMA((23,)),
            pltpu.SemaphoreType.DMA((6,)),
            pltpu.SemaphoreType.DMA((6,)),
            pltpu.SemaphoreType.DMA((n_lon,)),
            pltpu.SemaphoreType.DMA((n_lon,)),
        ]
    )
    anywhere = pl.BlockSpec(memory_space=pltpu.HBM)
    nu, nv = pl.pallas_call(
        functools.partial(kernel, n_lat, n_lon, L, R, C),
        out_shape=[jax.ShapeDtypeStruct(cube, f32)] * 2,
        in_specs=[anywhere] * 9,
        out_specs=[pl.BlockSpec(memory_space=pltpu.VMEM)] * 2,
        scratch_shapes=scratch,
        compiler_params=pltpu.CompilerParams(
            collective_id=0, has_side_effects=True, vmem_limit_bytes=60 * 1024 * 1024
        ),
    )(u, v, eu, ev, wu, wv, mu, mv, seam)
    return nu, nv


def solution(mesh):
    n_lat, n_lon = mesh.shape["lat"], mesh.shape["lon"]
    cube = P(None, "lat", "lon")
    flat = P("lat", "lon")
    return jax.shard_map(
        functools.partial(local, n_lat, n_lon),
        mesh=mesh,
        in_specs=(cube, cube, cube, cube, flat, flat, cube, cube, P()),
        out_specs=(cube, cube),
        check_vma=False,
    )
```

time: 144 us -> 45 us (0.31)
  the two profiles are of different devices: /device:TPU:129 before, /device:TPU:248 now
where the time goes in v1:
time: 45 us; the launch traced here: 44.5 us
  Pallas kernels  40.4 us (90%)
  local copies, waits for them, and re-layouts  3.48 us (8%)
  between operations  0.65 us (1%)
    pallas_call x1, Pallas kernels, local(): pl.pallas_call(functools.partial(kernel, n_lat, n_lon, L, R, C), out_shap...  40.4 us
    unnamed x4, local copies, waits for them, and re-layouts  3.48 us

profile of v1, /device:TPU:248, one launch (start us, length us, event | category | flops | bytes accessed | tf_op | source)
XLA Modules:
  0.0 44.5 jit_solution(2302783651725625208)
XLA Ops:
  0.6 40.4 %shard_map.104 = (f32[72,32,128]{2,1,0:T(8,128)}, f32[72,32,128]{2,1,0:T(8,128)}) custom-call(f32[72,32,128]{2,1,0:T(8,128)} %u.1, f32[72,32,128]{2,1,0:T(8,128)} %v.1, f32[72,32,128]{2,1,0:T(8,128)} %eu.1, f32[72,32,128]{2,1,0:T(8,128)} %ev.1, f32[32,128]{1,0:T(8,128)} %wu.1, f32[32,128]{1,0:T(8,128)} %wv.1, s32[72,32,128]{2,1,0:T(8,128)} %mu.1, ...), custom_call_target="tpu_custom_call" | custom-call | tf_op jit(solution)/shard_map/pallas_call | solution.py:376
  41.0 0.0 copy-start
  41.1 2.5 %copy.13 = f32[72,32,128]{2,1,0:T(8,128)} copy(f32[72,32,128]{2,1,0:T(8,128)} %get-tuple-element.4) | data formatting | bytes 2359296
  43.5 0.0 copy-done
  43.5 1.0 %copy.14 = f32[72,32,128]{2,1,0:T(8,128)} copy(f32[72,32,128]{2,1,0:T(8,128)S(1)} %copy-done) | data formatting | bytes 2359296
Async XLA Ops:
  41.0 2.5 %copy-start = (f32[72,32,128]{2,1,0:T(8,128)S(1)}, f32[72,32,128]{2,1,0:T(8,128)}, u32[]{:S(2)}) copy-start(f32[72,32,128]{2,1,0:T(8,128)} %get-tuple-element.5) | copy-start | bytes 3538948

commit v2 on v1

--- a/solution.py
+++ b/solution.py
@@ -18,7 +18,7 @@
     return pltpu.make_async_copy(src, dst, sem)
 
 
-def kernel(n_lat, n_lon, L, R, C, u, v, eu, ev, wu, wv, mu, mv, seam, ou, ov, *scratch):
+def kernel(n_lat, n_lon, L, R, C, tile, u, v, eu, ev, wu, wv, mu, mv, seam, ou, ov, *scratch):
     (
         us, vs, eus, evs, wus, wvs, mus, mvs, seams,
         pu, pv, pmu, pmv, peu, pev,
@@ -109,9 +109,8 @@
     CN[...] = jnp.concatenate([tv31, fill], axis=0).T[0:8, :]
     CS[...] = jnp.concatenate([SS[4], fill], axis=0).T[C - 8 : C, :]
 
-    pivot = seams[0] + 1
-    tile = pivot // C
-    turn = lax.rem(pivot, C)
+    turn = lax.rem(seams[0] + 1, C)
+    fold_peers = (lax.rem(tile + n_lon - lon, n_lon), lax.rem(tile + 2 * n_lon - 1 - lon, n_lon))
 
     @pl.when(jnp.logical_not(has_north))
     def _():
@@ -144,11 +143,25 @@
     to_northwest = send(CN, RCS, 4, lat + 1, west)
     to_southeast = send(CS, RCN, 5, lat - 1, east)
 
-    def fold_copy(k, slot):
+    def fold_copy(slot):
         return pltpu.make_async_remote_copy(
-            src_ref=SF, dst_ref=G.at[slot], send_sem=fold_send.at[k], recv_sem=fold_recv.at[slot],
-            device_id={"lat": lat, "lon": lax.rem(lon + k, n_lon)}, device_id_type=MESH,
+            src_ref=SF, dst_ref=G.at[slot], send_sem=fold_send.at[slot], recv_sem=fold_recv.at[slot],
+            device_id={"lat": lat, "lon": fold_peers[slot]}, device_id_type=MESH,
         )
+
+    def each_fold(act, own=None):
+        for slot in range(2):
+            mine = fold_peers[slot] == lon
+
+            @pl.when(jnp.logical_not(has_north | mine))
+            def _(slot=slot):
+                act(slot)
+
+            if own is not None:
+
+                @pl.when(jnp.logical_not(has_north) & mine)
+                def _(slot=slot):
+                    own(slot)
 
     @pl.when(has_north)
     def _():
@@ -160,10 +173,7 @@
         to_south.start()
         to_southeast.start()
 
-    @pl.when(jnp.logical_not(has_north))
-    def _():
-        for k in range(1, n_lon):
-            fold_copy(k, lon).start()
+    each_fold(lambda slot: fold_copy(slot).start())
 
     for copy in full_copies:
         copy.wait()
@@ -258,16 +268,16 @@
         first = stacked(((6, RCN[7:8, :]),))
         H[row_of(R), :] = jnp.concatenate([first, jnp.zeros((C - 8, C), f32)], axis=0).T[0:L, :]
 
+    def own_fold(slot):
+        G[slot] = SF[...]
+
+    each_fold(lambda slot: fold_copy(slot).wait_recv(), own_fold)
+
     @pl.when(jnp.logical_not(has_north))
     def _():
-        for k in range(1, n_lon):
-            fold_copy(k, lax.rem(lon + n_lon - k, n_lon)).wait_recv()
-        G[lon] = SF[...]
-        low = lax.rem(tile - lon + 2 * n_lon, n_lon)
-        high = lax.rem(tile - lon + 2 * n_lon - 1, n_lon)
         for i, (field, r) in enumerate(north):
-            field[row_of(R + r), :] = jnp.where(lane < turn, G[low, i], G[high, i])
-        H[row_of(R), :] = pltpu.roll(G[low, 4], 7, 1)
+            field[row_of(R + r), :] = jnp.where(lane < turn, G[0, i], G[1, i])
+        H[row_of(R), :] = pltpu.roll(G[0, 4], 7, 1)
 
     col = lax.broadcasted_iota(jnp.int32, (8, C), 1)
 
@@ -336,10 +346,7 @@
         to_south.wait_send()
         to_southeast.wait_send()
 
-    @pl.when(jnp.logical_not(has_north))
-    def _():
-        for k in range(1, n_lon):
-            fold_copy(k, lon).wait_send()
+    each_fold(lambda slot: fold_copy(slot).wait_send())
 
 
 def local(n_lat, n_lon, u, v, eu, ev, wu, wv, mu, mv, seam):
@@ -362,28 +369,33 @@
         + [vm((5, L, C), f32), vm((6, L, C), f32)]
         + [vm((5, L // 4, C), f32), vm((6, L // 4, C), f32)]
         + [vm((8, C), f32)] * 2
-        + [vm((n_lon, 6, L, C), f32)]
+        + [vm((2, 6, L, C), f32)]
         + [
             pltpu.SemaphoreType.DMA((6,)),
             pltpu.SemaphoreType.DMA((23,)),
             pltpu.SemaphoreType.DMA((6,)),
             pltpu.SemaphoreType.DMA((6,)),
-            pltpu.SemaphoreType.DMA((n_lon,)),
-            pltpu.SemaphoreType.DMA((n_lon,)),
+            pltpu.SemaphoreType.DMA((2,)),
+            pltpu.SemaphoreType.DMA((2,)),
         ]
     )
     anywhere = pl.BlockSpec(memory_space=pltpu.HBM)
-    nu, nv = pl.pallas_call(
-        functools.partial(kernel, n_lat, n_lon, L, R, C),
-        out_shape=[jax.ShapeDtypeStruct(cube, f32)] * 2,
-        in_specs=[anywhere] * 9,
-        out_specs=[pl.BlockSpec(memory_space=pltpu.VMEM)] * 2,
-        scratch_shapes=scratch,
-        compiler_params=pltpu.CompilerParams(
-            collective_id=0, has_side_effects=True, vmem_limit_bytes=60 * 1024 * 1024
-        ),
-    )(u, v, eu, ev, wu, wv, mu, mv, seam)
-    return nu, nv
+
+    def step(tile, *operands):
+        return pl.pallas_call(
+            functools.partial(kernel, n_lat, n_lon, L, R, C, tile),
+            out_shape=[jax.ShapeDtypeStruct(cube, f32)] * 2,
+            in_specs=[anywhere] * 9,
+            out_specs=[pl.BlockSpec(memory_space=pltpu.VMEM)] * 2,
+            scratch_shapes=scratch,
+            compiler_params=pltpu.CompilerParams(
+                collective_id=tile, has_side_effects=True, vmem_limit_bytes=32 * 1024 * 1024
+            ),
+        )(*(pltpu.with_memory_space_constraint(x, pltpu.HBM) for x in operands))
+
+    tile = lax.rem((seam[0] + 1) // C, n_lon)
+    branches = [functools.partial(step, t) for t in range(n_lon)]
+    return tuple(lax.switch(tile, branches, u, v, eu, ev, wu, wv, mu, mv, seam))
 
 
 def solution(mesh):

time: 45 us -> 36.7 us (0.82)
  Pallas kernels: 40.4 us -> 31.8 us
  between operations: 0.65 us -> 1.32 us
    pallas_call x1, Pallas kernels: 40.4 us -> 31.8 us  [step(): pl.pallas_call(functools.partial(kernel, n_lat, n_lon, L, R, C, tile), ou...]
    unnamed x4 -> x2, local copies, waits for them, and re-layouts: 3.48 us -> 2.03 us
    slice x0 -> x1, local copies, waits for them, and re-layouts: none -> 1.2 us  [local(): tile = lax.rem((seam[0] + 1) // C, n_lon)]
where the time goes in v2:
time: 36.7 us; the launch traced here: 36.4 us
  Pallas kernels  31.8 us (87%)
  local copies, waits for them, and re-layouts  3.23 us (9%)
  between operations  1.32 us (4%)
    pallas_call x1, Pallas kernels, step(): pl.pallas_call(functools.partial(kernel, n_lat, n_lon, L, R, C, tile), ou...  31.8 us
    unnamed x2, local copies, waits for them, and re-layouts  2.03 us
    slice x1, local copies, waits for them, and re-layouts, local(): tile = lax.rem((seam[0] + 1) // C, n_lon)  1.2 us

profile of v2, /device:TPU:248, one launch (start us, length us, event | category | flops | bytes accessed | tf_op | source)
XLA Modules:
  0.0 36.4 jit_solution(7433692292138243675)
XLA Ops:
  0.6 1.2 %slice.3 = s32[1]{0:T(128)} slice(s32[1024]{0:T(1024)} %param.25), slice={[0:1]} | slice | bytes 8 | tf_op jit(solution)/shard_map/slice | solution.py:396
  2.5 31.8 %conditional.1 = ((f32[72,32,128]{2,1,0:T(8,128)S(1)}, f32[72,32,128]{2,1,0:T(8,128)S(1)})) conditional(s32[]{:T(128)} %clamp.3, (f32[72,32,128]{2,1,0:T(8,128)}, f32[72,32,128]{2,1,0:T(8,128)}, f32[72,32,128]{2,1,0:T(8,128)}, f32[72,32,128]{2,1,0:T(8,128)}, f32[32,128]{1,0:T(8,128)}, /*index=5*/f32[32,128]{1,0:T(8,128)}, ...), branch_computations={%region_0.1_spmd, %region_1.2_spmd, %region_2.3_spmd, %region_3.4_... | conditional | bytes 8 | solution.py:398
  2.5 31.8 %branch_1_fun.1 = (f32[72,32,128]{2,1,0:T(8,128)S(1)}, f32[72,32,128]{2,1,0:T(8,128)S(1)}) custom-call(f32[72,32,128]{2,1,0:T(8,128)} %get-tuple-element.153.u, f32[72,32,128]{2,1,0:T(8,128)} %get-tuple-element.154.v, f32[72,32,128]{2,1,0:T(8,128)} %get-tuple-element.155.eu, f32[72,32,128]{2,1,0:T(8,128)} %get-tuple-element.156.ev, ...), custom_call_target="tpu_custom_call" | custom-call | tf_op jit(solution)/shard_map/cond/branch_1_fun/pallas_call | solution.py:385
  34.4 1.0 %copy.45 = f32[72,32,128]{2,1,0:T(8,128)} copy(f32[72,32,128]{2,1,0:T(8,128)S(1)} %get-tuple-element.254) | data formatting | bytes 2359296
  35.4 1.0 %copy.46 = f32[72,32,128]{2,1,0:T(8,128)} copy(f32[72,32,128]{2,1,0:T(8,128)S(1)} %get-tuple-element.255) | data formatting | bytes 2359296

commit v3 on v2

v3 whole, which is shorter than its diff:
```python
import functools

import jax
import jax.numpy as jnp
from jax import lax
from jax.experimental import pallas as pl
from jax.experimental.pallas import tpu as pltpu
from jax.sharding import PartitionSpec as P

MESH = pl.DeviceIdType.MESH
f32 = jnp.float32

FACTOR = 0.2 * 0.5 / 12.0


U_COLS = {126: 0, 127: 1, 0: 5, 1: 6, 124: 11, 125: 12, 2: 13, 3: 14}
V_COLS = {126: 2, 127: 3, 0: 7, 1: 8, 124: 15, 125: 16, 2: 17, 3: 18}
T_COLS = {127: 4, 0: 9, 125: 19, 126: 20, 1: 21, 2: 22}
S_COLS = {0: 10, 126: 23, 127: 24, 1: 25, 2: 26}
OWN = 27
U_AT, V_AT, T_AT, S_AT = 0, 8, 15, 20


def q(a, b, c, d):
    return 7.0 * (b + c) - (a + d)


def roll(x, shift):
    return pltpu.roll(x, shift % x.shape[1], 1)


def kernel(n_lat, n_lon, L, R, C, LC, tile, u, v, eu, ev, wu, wv, mu, mv, seam, ou, ov, *scratch):
    (
        us, vs, eus, evs, wus, wvs, mus, mvs, seams,
        pu, pv, pmu, pmv, peu, pev,
        UM, VM, TU, TV, TS,
        SN, SS, SF, CN, CS,
        RS, RN, RCS, RCN, G, KS, KN,
        TO, TC, TX, RW, RE, HP,
        in_sem, row_sem, send_sem, recv_sem, fold_send, fold_recv, lon_send, lon_recv,
    ) = scratch
    lat = lax.axis_index("lat")
    lon = lax.axis_index("lon")
    east = lax.rem(lon + 1, n_lon)
    west = lax.rem(lon + n_lon - 1, n_lon)
    has_north = lat < n_lat - 1
    has_south = lat > 0
    pitch = R + 8
    chunks = L // LC
    GB = LC // 4

    rows = (0, 1, R - 2, R - 1)
    loads = [(wu, wus), (wv, wvs), (seam, seams)]
    for src, dst in ((u, pu), (mu, pmu), (v, pv), (mv, pmv), (eu, peu), (ev, pev)):
        for i, r in enumerate(rows):
            loads.append((src.at[:, r, :], dst.at[i]))
    row_copies = [pltpu.make_async_copy(s, d, row_sem.at[i]) for i, (s, d) in enumerate(loads)]
    fields = ((u, us), (mu, mus), (v, vs), (mv, mvs), (eu, eus), (ev, evs))
    full_copies = [
        [
            pltpu.make_async_copy(s.at[pl.ds(c * LC, LC)], d.at[pl.ds(c * LC, LC)], in_sem.at[c, i])
            for i, (s, d) in enumerate(fields)
        ]
        for c in range(chunks)
    ]
    for copy in row_copies:
        copy.start()
    for group in full_copies:
        for copy in group:
            copy.start()

    barrier = pltpu.get_barrier_semaphore()

    def greet(a, b):
        pl.semaphore_signal(barrier, inc=1, device_id={"lat": a, "lon": b}, device_id_type=MESH)

    greet(lat, east)
    greet(lat, west)

    @pl.when(has_north)
    def _():
        greet(lat + 1, lon)
        greet(lat + 1, west)

    @pl.when(has_south)
    def _():
        greet(lat - 1, lon)
        greet(lat - 1, east)

    @pl.when(jnp.logical_not(has_north))
    def _():
        for k in range(2, n_lon - 1):
            greet(lat, lax.rem(lon + k, n_lon))

    for copy in row_copies:
        copy.wait()

    lane = lax.broadcasted_iota(jnp.int32, (L, C), 1)
    um0 = pmu[0].astype(f32) * pu[0]
    um1 = pmu[1].astype(f32) * pu[1]
    vm0 = pmv[0].astype(f32) * pv[0]
    vm1 = pmv[1].astype(f32) * pv[1]
    tu0 = wus[0:1, :] * peu[0] * um0
    SS[0] = um0
    SS[1] = um1
    SS[2] = vm0
    SS[3] = vm1
    SS[4] = tu0
    SS[5] = wvs[0:1, :] * pev[0] * vm0
    um30 = pmu[2].astype(f32) * pu[2]
    um31 = pmu[3].astype(f32) * pu[3]
    vm30 = pmv[2].astype(f32) * pv[2]
    vm31 = pmv[3].astype(f32) * pv[3]
    tv31 = wvs[R - 1 : R, :] * pev[3] * vm31
    SN[0] = um30
    SN[1] = um31
    SN[2] = vm30
    SN[3] = vm31
    SN[4] = tv31
    fill = jnp.zeros((C - L, C), f32)
    CN[...] = jnp.concatenate([tv31, fill], axis=0).T[0:8, :]
    CS[...] = jnp.concatenate([tu0, fill], axis=0).T[C - 8 : C, :]

    turn = lax.rem(seams[0] + 1, C)
    fold_peers = (lax.rem(tile + n_lon - lon, n_lon), lax.rem(tile + 2 * n_lon - 1 - lon, n_lon))

    @pl.when(jnp.logical_not(has_north))
    def _():
        index = (turn + (2 * C - 1) - lane) & (C - 1)
        tu31 = wus[R - 1 : R, :] * peu[3] * um31
        for i, plane in enumerate((um31, um30, vm31, vm30, tu31, tv31)):
            SF[i] = -jnp.take_along_axis(plane, index, axis=1)

    @pl.when(has_north & has_south)
    def _():
        pl.semaphore_wait(barrier, 6)

    @pl.when(jnp.logical_not(has_south))
    def _():
        pl.semaphore_wait(barrier, 4)

    @pl.when(jnp.logical_not(has_north))
    def _():
        pl.semaphore_wait(barrier, n_lon + 1)

    def send(src, dst, i, a, b):
        return pltpu.make_async_remote_copy(
            src_ref=src, dst_ref=dst, send_sem=send_sem.at[i], recv_sem=recv_sem.at[i],
            device_id={"lat": a, "lon": b}, device_id_type=MESH,
        )

    def send_columns(src, dst, c, i, b):
        return pltpu.make_async_remote_copy(
            src_ref=src, dst_ref=dst, send_sem=lon_send.at[c, i], recv_sem=lon_recv.at[c, i],
            device_id={"lat": lat, "lon": b}, device_id_type=MESH,
        )

    to_north = send(SN, RS, 0, lat + 1, lon)
    to_south = send(SS, RN, 1, lat - 1, lon)
    to_northwest = send(CN, RCS, 2, lat + 1, west)
    to_southeast = send(CS, RCN, 3, lat - 1, east)
    to_east = [send_columns(TO.at[c, 0:5], RW.at[c], c, 0, east) for c in range(chunks)]
    to_west = [send_columns(TO.at[c, 5:11], RE.at[c], c, 1, west) for c in range(chunks)]

    def fold_copy(slot):
        return pltpu.make_async_remote_copy(
            src_ref=SF, dst_ref=G.at[slot], send_sem=fold_send.at[slot], recv_sem=fold_recv.at[slot],
            device_id={"lat": lat, "lon": fold_peers[slot]}, device_id_type=MESH,
        )

    def each_fold(act, own=None):
        for slot in range(2):
            mine = fold_peers[slot] == lon

            @pl.when(jnp.logical_not(has_north | mine))
            def _(slot=slot):
                act(slot)

            if own is not None:

                @pl.when(jnp.logical_not(has_north) & mine)
                def _(slot=slot):
                    own(slot)

    @pl.when(has_north)
    def _():
        to_north.start()
        to_northwest.start()

    @pl.when(has_south)
    def _():
        to_south.start()
        to_southeast.start()

    each_fold(lambda slot: fold_copy(slot).start())

    lanes = lax.broadcasted_iota(jnp.int32, (4 * R, C), 1)
    wide_u = jnp.concatenate([wus[...]] * 4, axis=0)
    wide_v = jnp.concatenate([wvs[...]] * 4, axis=0)

    def level_rows(k, o=0):
        return pl.ds(pl.multiple_of(k * pitch + 8, 8) + o, R)

    def pack(c, g):
        first = c * LC + 4 * g

        def whole(ref):
            return ref[pl.ds(first, 4)].reshape(4 * R, C)

        um = whole(mus).astype(f32) * whole(us)
        vm = whole(mvs).astype(f32) * whole(vs)
        tu = wide_u * whole(eus) * um
        tv = wide_v * whole(evs) * vm
        for i in range(4):
            part = slice(i * R, (i + 1) * R)
            to = level_rows(first + i)
            UM[to, :] = um[part]
            VM[to, :] = vm[part]
            TU[to, :] = tu[part]
            TV[to, :] = tv[part]
        both = jnp.where((lanes >= 4) & (lanes <= 11), roll(vm, V_AT), um)
        both = jnp.where((lanes >= 12) & (lanes <= 17), roll(tu, T_AT), both)
        both = jnp.where((lanes >= 18) & (lanes <= 22), roll(tv, S_AT), both)
        turned = both.T
        for at, columns in ((U_AT, U_COLS), (V_AT, V_COLS), (T_AT, T_COLS), (S_AT, S_COLS)):
            for column, row in columns.items():
                r = (column + at) % C
                TO[c, row, pl.ds(g, 1), :] = turned[r : r + 1, :]

    per = 3 if GB % 3 == 0 else 2
    for c in range(chunks):
        for copy in full_copies[c]:
            copy.wait()

        def some(h, carry, c=c):
            for i in range(per):
                pack(c, h * per + i)
            return carry

        lax.fori_loop(0, GB // per, some, 0)
        to_east[c].start()
        to_west[c].start()

    def sums(k, carry):
        at = pl.ds(pl.multiple_of(k * pitch * 4 + 8, 8), pitch * 4)
        tv = TV[at, :]
        TS[at, :] = tv + roll(tv, -1)
        return carry

    lax.fori_loop(0, L // 4, sums, 0)

    at_lane = lanes[0 : 4 * R]

    def step(k):
        def get(ref, o):
            return ref[level_rows(k, o), :]

        u0, v0, t0, t1 = get(UM, 0), get(VM, 0), get(TU, 0), get(TU, 1)
        a1, a2, b1, b2 = roll(u0, 1), roll(u0, 2), roll(u0, -1), roll(u0, -2)
        tl, tr = roll(t0, 1), roll(t0, -1)
        c1, c2, d1, d2 = roll(v0, 1), roll(v0, 2), roll(v0, -1), roll(v0, -2)
        ts = t0 + t1
        tsl = roll(ts, 1)
        um2, um1, up1, up2 = (get(UM, o) for o in (-2, -1, 1, 2))
        vm2, vm1, vp1, vp2 = (get(VM, o) for o in (-2, -1, 1, 2))
        sm, s0, sp = get(TV, -1), get(TV, 0), get(TV, 1)
        cu = mus[k].astype(f32) * FACTOR / (wus[...] * eus[k])
        cv = mvs[k].astype(f32) * FACTOR / (wvs[...] * evs[k])
        du = get(TS, 0) * q(um1, u0, up1, up2) - get(TS, -1) * q(um2, um1, u0, up1)
        dv = (s0 + sp) * q(vm1, v0, vp1, vp2) - (sm + s0) * q(vm2, vm1, v0, vp1)
        du = du + ((t0 + tr) * q(a1, u0, b1, b2) - (tl + t0) * q(a2, a1, u0, b1))
        dv = dv + (ts * q(c1, v0, d1, d2) - tsl * q(c2, c1, v0, d1))
        ou[k] = u0 - cu * du
        ov[k] = v0 - cv * dv
        return cu, cv

    def steps(c, g):
        done = [step(c * LC + 4 * g + i) for i in range(4)]
        cu = jnp.concatenate([d[0] for d in done], axis=0)
        cv = jnp.concatenate([d[1] for d in done], axis=0)
        turned = jnp.where((lanes >= 2) & (lanes <= 5), roll(cv, 4), cu).T
        for row, r in enumerate((C - 2, C - 1, 0, 1, 2, 3, 4, 5)):
            TC[c, row, pl.ds(g, 1), :] = turned[r : r + 1, :]

    def two(h, carry):
        for i in range(2):
            steps(lax.div(h, GB // 2), lax.rem(h, GB // 2) * 2 + i)
        return carry

    lax.fori_loop(0, L // 8, two, 0)

    def edge(x, y, t, s, cu, cv):
        def up(z, o):
            return roll(z, -o)

        f = [(t[a] + t[a + 1]) * q(*x[a : a + 4]) for a in range(3)]
        g = [(t[a] + up(t[a], 1)) * q(*y[a : a + 4]) for a in range(3)]
        out_u, out_v = [], []
        for i in range(2):
            xc, yc = x[i + 2], y[i + 2]
            F = (s[i] + s[i + 1]) * q(up(xc, -1), xc, up(xc, 1), up(xc, 2))
            E = (up(s[i], -1) + s[i]) * q(up(yc, -2), up(yc, -1), yc, up(yc, 1))
            out_u.append(xc - cu[i] * ((f[i + 1] - f[i]) + (F - up(F, -1))))
            out_v.append(yc - cv[i] * ((g[i + 1] - g[i]) + (up(E, 1) - E)))
        return out_u, out_v

    sub = lax.broadcasted_iota(jnp.int32, (8, C), 0)

    def stacked(parts):
        out = jnp.zeros((8, C), f32)
        for r, row in parts:
            out = jnp.where(sub == r, jnp.broadcast_to(row, (8, C)), out)
        return out

    in_edge = (lanes <= 1) | (lanes >= C - 2)

    def unpack(c, g):
        at = pl.ds(g, 1)
        x = [TX[c, i, at, :] for i in range(8)]
        w = [RW[c, f, at, :] for f in range(5)]
        e = [RE[c, f, at, :] for f in range(6)]
        low = stacked(list(enumerate((x[2], x[3], x[4], x[5], x[6], x[7], w[4], e[4]))))
        mid = stacked(list(enumerate((w[0], w[1], e[0], e[1], w[2], w[3], e[2], e[3]))))
        top = stacked(((5, e[5]), (6, x[0]), (7, x[1])))
        turned = jnp.concatenate([low, mid, jnp.zeros((C - 24, C), f32), top], axis=0).T
        first = c * LC + 4 * g
        to = pl.ds(first, 4)
        ou[to] = jnp.where(in_edge, turned, ou[to].reshape(4 * R, C)).reshape(4, R, C)
        ov[to] = jnp.where(in_edge, roll(turned, -4), ov[to].reshape(4 * R, C)).reshape(4, R, C)
        for i in range(4):
            for j, r in enumerate((0, 1, 2, R - 3, R - 2, R - 1)):
                HP[j, pl.ds(first + i, 1), :] = turned[i * R + r : i * R + r + 1, :]

    for c in range(chunks):
        to_east[c].wait_recv()
        to_west[c].wait_recv()
        own = {
            name: (lambda column, table=table: TO[c, table[column]])
            for name, table in (("u", U_COLS), ("v", V_COLS), ("t", T_COLS), ("s", S_COLS))
        }
        eu_, ev_ = edge(
            [own["u"](i) for i in (124, 125, 126, 127)] + [RE[c, 0], RE[c, 1]],
            [own["v"](i) for i in (124, 125, 126, 127)] + [RE[c, 2], RE[c, 3]],
            [own["t"](i) for i in (125, 126, 127)] + [RE[c, 4]],
            [own["s"](i) for i in (126, 127)] + [RE[c, 5]],
            (TC[c, 0], TC[c, 1]), (TC[c, 4], TC[c, 5]),
        )
        wu_, wv_ = edge(
            [RW[c, 0], RW[c, 1]] + [own["u"](i) for i in (0, 1, 2, 3)],
            [RW[c, 2], RW[c, 3]] + [own["v"](i) for i in (0, 1, 2, 3)],
            [RW[c, 4]] + [own["t"](i) for i in (0, 1, 2)],
            [own["s"](i) for i in (0, 1, 2)],
            (TC[c, 2], TC[c, 3]), (TC[c, 6], TC[c, 7]),
        )
        for i, value in enumerate(eu_ + wu_ + ev_ + wv_):
            TX[c, i] = value

        def several(h, carry, c=c):
            for i in range(per):
                unpack(c, h * per + i)
            return carry

        lax.fori_loop(0, GB // per, several, 0)

    @pl.when(has_south)
    def _():
        to_north.wait_recv()
        to_northwest.wait_recv()
        last = stacked(((0, RCS[0:1, :]),))
        KS[...] = jnp.concatenate([last, jnp.zeros((C - 8, C), f32)], axis=0).T[0:L, :]

    @pl.when(jnp.logical_not(has_south))
    def _():
        RS[...] = jnp.zeros_like(RS)
        KS[...] = jnp.zeros_like(KS)

    @pl.when(has_north)
    def _():
        to_south.wait_recv()
        to_southeast.wait_recv()
        first = stacked(((7, RCN[7:8, :]),))
        KN[...] = jnp.concatenate([jnp.zeros((C - 8, C), f32), first], axis=0).T[0:L, :]

    def own_fold(slot):
        G[slot] = SF[...]

    each_fold(lambda slot: fold_copy(slot).wait_recv(), own_fold)

    @pl.when(jnp.logical_not(has_north))
    def _():
        for i in range(6):
            RN[i] = jnp.where(lane < turn, G[0, i], G[1, i])
        KN[...] = G[0, 4]

    col = lax.broadcasted_iota(jnp.int32, (LC, C), 1)

    def left1(x, h):
        return roll(jnp.where(col == C - 1, h, x), 1)

    def left2(x, h):
        return roll(jnp.where(col >= C - 2, h, x), 2)

    def right1(x, h):
        return roll(jnp.where(col == 0, h, x), -1)

    def right2(x, h):
        return roll(jnp.where(col <= 1, h, x), -2)

    def edge_rows(c, carry):
        part = pl.ds(pl.multiple_of(c * LC, 8), LC)

        def own(ref, r):
            return ref[pl.ds(c * LC * pitch + 8 + r, LC, stride=pitch), :]

        def halo(j, shift):
            return roll(HP[j, part, :], shift)

        south = (
            [RS[0, part, :], RS[1, part, :]] + [own(UM, r) for r in range(4)],
            [RS[2, part, :], RS[3, part, :]] + [own(VM, r) for r in range(4)],
            [own(TU, r) for r in range(3)],
            [RS[4, part, :]] + [own(TV, r) for r in range(3)],
            [halo(j, -7) for j in range(3)],
            [KS[part, :], halo(0, 3), halo(1, 3)],
        )
        north = (
            [own(UM, R - 4 + r) for r in range(4)] + [RN[0, part, :], RN[1, part, :]],
            [own(VM, R - 4 + r) for r in range(4)] + [RN[2, part, :], RN[3, part, :]],
            [own(TU, R - 2), own(TU, R - 1), RN[4, part, :]],
            [own(TV, R - 3 + r) for r in range(3)] + [RN[5, part, :]],
            [halo(4, -7), halo(5, -7), KN[part, :]],
            [halo(3, 3), halo(4, 3), halo(5, 3)],
        )
        for side, (x, y, t, s, ht, hs) in enumerate((south, north)):
            F = [(s[a] + right1(s[a], hs[a])) * q(*x[a : a + 4]) for a in range(3)]
            E = [(s[a] + s[a + 1]) * q(*y[a : a + 4]) for a in range(3)]
            for i in range(2):
                p = 2 * side + i
                r = rows[p]
                xc, yc = x[i + 2], y[i + 2]
                hu, hv = halo((0, 1, 4, 5)[p], -10), halo((0, 1, 4, 5)[p], -14)
                a1, a2, b1, b2 = left1(xc, hu), left2(xc, hu), right1(xc, hu), right2(xc, hu)
                c1, c2, d1, d2 = left1(yc, hv), left2(yc, hv), right1(yc, hv), right2(yc, hv)
                du = (t[i] + right1(t[i], ht[i])) * q(a1, xc, b1, b2)
                du = du - (left1(t[i], ht[i]) + t[i]) * q(a2, a1, xc, b1)
                ts, th = t[i] + t[i + 1], ht[i] + ht[i + 1]
                dv = ts * q(c1, yc, d1, d2) - left1(ts, th) * q(c2, c1, yc, d1)
                du = du + (F[i + 1] - F[i])
                dv = dv + (E[i + 1] - E[i])
                cu = pmu[p, part, :].astype(f32) * FACTOR / (wus[r : r + 1, :] * peu[p, part, :])
                cv = pmv[p, part, :].astype(f32) * FACTOR / (wvs[r : r + 1, :] * pev[p, part, :])
                ou[part, r, :] = xc - cu * du
                ov[part, r, :] = yc - cv * dv
        return carry

    lax.fori_loop(0, chunks, edge_rows, 0)

    for c in range(chunks):
        to_east[c].wait_send()
        to_west[c].wait_send()

    @pl.when(has_north)
    def _():
        to_north.wait_send()
        to_northwest.wait_send()

    @pl.when(has_south)
    def _():
        to_south.wait_send()
        to_southeast.wait_send()

    each_fold(lambda slot: fold_copy(slot).wait_send())


def local(n_lat, n_lon, u, v, eu, ev, wu, wv, mu, mv, seam):
    L, R, C = u.shape
    cube = (L, R, C)
    LC = 24 if L % 24 == 0 else 8
    chunks, GB = L // LC, LC // 4
    vm = pltpu.VMEM
    dma = pltpu.SemaphoreType.DMA
    scratch = (
        [vm(cube, f32)] * 4
        + [vm((R, C), f32)] * 2
        + [vm(cube, jnp.int32)] * 2
        + [pltpu.SMEM(seam.shape, jnp.int32)]
        + [vm((4, L, C), f32)] * 2
        + [vm((4, L, C), jnp.int32)] * 2
        + [vm((4, L, C), f32)] * 2
        + [vm((L * (R + 8) + 16, C), f32)] * 5
        + [vm((5, L, C), f32), vm((6, L, C), f32), vm((6, L, C), f32)]
        + [vm((8, C), f32)] * 2
        + [vm((5, L, C), f32), vm((6, L, C), f32)]
        + [vm((8, C), f32)] * 2
        + [vm((2, 6, L, C), f32)]
        + [vm((L, C), f32)] * 2
        + [vm((chunks, OWN, GB, C), f32), vm((chunks, 8, GB, C), f32), vm((chunks, 8, GB, C), f32)]
        + [vm((chunks, 5, GB, C), f32), vm((chunks, 6, GB, C), f32)]
        + [vm((6, L, C), f32)]
        + [dma((chunks, 6)), dma((27,)), dma((4,)), dma((4,)), dma((2,)), dma((2,)), dma((chunks, 2)), dma((chunks, 2))]
    )
    hbm = pl.BlockSpec(memory_space=pltpu.HBM)

    def step(tile, *operands):
        return pl.pallas_call(
            functools.partial(kernel, n_lat, n_lon, L, R, C, LC, tile),
            out_shape=[jax.ShapeDtypeStruct(cube, f32)] * 2,
            in_specs=[hbm] * 9,
            out_specs=[pl.BlockSpec(memory_space=pltpu.VMEM)] * 2,
            scratch_shapes=scratch,
            compiler_params=pltpu.CompilerParams(
                collective_id=tile, has_side_effects=True, vmem_limit_bytes=32 * 1024 * 1024
            ),
        )(*(pltpu.with_memory_space_constraint(x, pltpu.HBM) for x in operands))

    tile = lax.rem((seam[0] + 1) // C, n_lon)
    branches = [functools.partial(step, t) for t in range(n_lon)]
    return tuple(lax.switch(tile, branches, u, v, eu, ev, wu, wv, mu, mv, seam))


def solution(mesh):
    n_lat, n_lon = mesh.shape["lat"], mesh.shape["lon"]
    cube = P(None, "lat", "lon")
    flat = P("lat", "lon")
    return jax.shard_map(
        functools.partial(local, n_lat, n_lon),
        mesh=mesh,
        in_specs=(cube, cube, cube, cube, flat, flat, cube, cube, P()),
        out_specs=(cube, cube),
        check_vma=False,
    )
```

time: 36.7 us -> 25.7 us (0.70)
  the two profiles are of different devices: /device:TPU:248 before, /device:TPU:105 now
where the time goes in v3:
time: 25.7 us; the launch traced here: 25.5 us
  Pallas kernels  20.4 us (79%)
  local copies, waits for them, and re-layouts  3.23 us (13%)
  between operations  1.32 us (5%)
  loops' own time  0.57 us (2%)
    pallas_call x1, Pallas kernels, step(): pl.pallas_call(functools.partial(kernel, n_lat, n_lon, L, R, C, LC, tile)...  20.4 us
    unnamed x2, local copies, waits for them, and re-layouts  2.03 us
    slice x1, local copies, waits for them, and re-layouts, local(): tile = lax.rem((seam[0] + 1) // C, n_lon)  1.2 us
    another operation x1, loops' own time, local(): return tuple(lax.switch(tile, branches, u, v, eu, ev, wu, wv, mu, mv, seam))  0.57 us

profile of v3, /device:TPU:105, one launch (start us, length us, event | category | flops | bytes accessed | tf_op | source)
XLA Modules:
  0.0 25.5 jit_solution(16849908078995112742)
XLA Ops:
  0.6 1.2 %slice.3 = s32[1]{0:T(128)} slice(s32[1024]{0:T(1024)} %param.25), slice={[0:1]} | slice | bytes 8 | tf_op jit(solution)/shard_map/slice | solution.py:516
  2.5 21.0 %conditional.1 = ((f32[72,32,128]{2,1,0:T(8,128)S(1)}, f32[72,32,128]{2,1,0:T(8,128)S(1)})) conditional(s32[]{:T(128)} %clamp.3, (f32[72,32,128]{2,1,0:T(8,128)}, f32[72,32,128]{2,1,0:T(8,128)}, f32[72,32,128]{2,1,0:T(8,128)}, f32[72,32,128]{2,1,0:T(8,128)}, f32[32,128]{1,0:T(8,128)}, /*index=5*/f32[32,128]{1,0:T(8,128)}, ...), branch_computations={%region_0.1_spmd, %region_1.2_spmd, %region_2.3_spmd, %region_3.4_... | conditional | bytes 8 | solution.py:518
  2.8 20.4 %branch_5_fun.1 = (f32[72,32,128]{2,1,0:T(8,128)S(1)}, f32[72,32,128]{2,1,0:T(8,128)S(1)}) custom-call(f32[72,32,128]{2,1,0:T(8,128)} %get-tuple-element.189.u, f32[72,32,128]{2,1,0:T(8,128)} %get-tuple-element.190.v, f32[72,32,128]{2,1,0:T(8,128)} %get-tuple-element.191.eu, f32[72,32,128]{2,1,0:T(8,128)} %get-tuple-element.192.ev, ...), custom_call_target="tpu_custom_call" | custom-call | tf_op jit(solution)/shard_map/cond/branch_5_fun/pallas_call | solution.py:505
  23.5 1.0 %copy.45 = f32[72,32,128]{2,1,0:T(8,128)} copy(f32[72,32,128]{2,1,0:T(8,128)S(1)} %get-tuple-element.254) | data formatting | bytes 2359296
  24.5 1.0 %copy.46 = f32[72,32,128]{2,1,0:T(8,128)} copy(f32[72,32,128]{2,1,0:T(8,128)S(1)} %get-tuple-element.255) | data formatting | bytes 2359296

commit v4 on v3

v4 whole, which is shorter than its diff:
```python
import functools

import jax
import jax.numpy as jnp
from jax import lax
from jax.experimental import pallas as pl
from jax.experimental.pallas import tpu as pltpu
from jax.sharding import PartitionSpec as P

MESH = pl.DeviceIdType.MESH
f32 = jnp.float32

FACTOR = 0.2 * 0.5 / 12.0


EAST = (("U", 126), ("U", 127), ("V", 126), ("V", 127), ("T", 127))
WEST = (("U", 0), ("U", 1), ("V", 0), ("V", 1), ("T", 0), ("S", 0))


def q(a, b, c, d):
    return 7.0 * (b + c) - (a + d)


TP = 144


def roll(x, shift):
    return pltpu.roll(x, shift % x.shape[1], 1)


def kernel(n_lat, n_lon, L, R, C, LC, tile, u, v, eu, ev, wu, wv, mu, mv, seam, ou, ov, *scratch):
    (
        us, vs, eus, evs, wus, wvs, mus, mvs, seams,
        pu, pv, pmu, pmv, peu, pev,
        UM, VM, TU, TV, TS, QA, QB, DV, CU, CV,
        UT, VT, TT, ST, XT, UT2, VT2, FX, GX,
        SN, SS, SF, CN, CS,
        RS, RN, RCS, RCN, G, KS, KN,
        TO, RW, RE,
        in_sem, row_sem, send_sem, recv_sem, fold_send, fold_recv, lon_send, lon_recv,
    ) = scratch
    lat = lax.axis_index("lat")
    lon = lax.axis_index("lon")
    east = lax.rem(lon + 1, n_lon)
    west = lax.rem(lon + n_lon - 1, n_lon)
    has_north = lat < n_lat - 1
    has_south = lat > 0
    pitch = R + 8
    chunks = L // LC
    GB = LC // 4

    rows = (0, 1, R - 2, R - 1)
    loads = [(wu, wus), (wv, wvs), (seam, seams)]
    for src, dst in ((u, pu), (mu, pmu), (v, pv), (mv, pmv), (eu, peu), (ev, pev)):
        for i, r in enumerate(rows):
            loads.append((src.at[:, r, :], dst.at[i]))
    row_copies = [pltpu.make_async_copy(s, d, row_sem.at[i]) for i, (s, d) in enumerate(loads)]
    fields = ((u, us), (mu, mus), (v, vs), (mv, mvs), (eu, eus), (ev, evs))
    full_copies = [
        [
            pltpu.make_async_copy(s.at[pl.ds(c * LC, LC)], d.at[pl.ds(c * LC, LC)], in_sem.at[c, i])
            for i, (s, d) in enumerate(fields)
        ]
        for c in range(chunks)
    ]
    for copy in row_copies:
        copy.start()

    barrier = pltpu.get_barrier_semaphore()

    def greet(a, b):
        pl.semaphore_signal(barrier, inc=1, device_id={"lat": a, "lon": b}, device_id_type=MESH)

    greet(lat, east)
    greet(lat, west)

    @pl.when(has_north)
    def _():
        greet(lat + 1, lon)
        greet(lat + 1, west)

    @pl.when(has_south)
    def _():
        greet(lat - 1, lon)
        greet(lat - 1, east)

    @pl.when(jnp.logical_not(has_north))
    def _():
        for k in range(2, n_lon - 1):
            greet(lat, lax.rem(lon + k, n_lon))

    for copy in row_copies:
        copy.wait()
    for group in full_copies:
        for copy in group:
            copy.start()

    lane = lax.broadcasted_iota(jnp.int32, (L, C), 1)
    um0 = pmu[0].astype(f32) * pu[0]
    um1 = pmu[1].astype(f32) * pu[1]
    vm0 = pmv[0].astype(f32) * pv[0]
    vm1 = pmv[1].astype(f32) * pv[1]
    tu0 = wus[0:1, :] * peu[0] * um0
    SS[0] = um0
    SS[1] = um1
    SS[2] = vm0
    SS[3] = vm1
    SS[4] = tu0
    SS[5] = wvs[0:1, :] * pev[0] * vm0
    um30 = pmu[2].astype(f32) * pu[2]
    um31 = pmu[3].astype(f32) * pu[3]
    vm30 = pmv[2].astype(f32) * pv[2]
    vm31 = pmv[3].astype(f32) * pv[3]
    tv31 = wvs[R - 1 : R, :] * pev[3] * vm31
    SN[0] = um30
    SN[1] = um31
    SN[2] = vm30
    SN[3] = vm31
    SN[4] = tv31
    fill = jnp.zeros((C - L, C), f32)
    CN[...] = jnp.concatenate([tv31, fill], axis=0).T[0:8, :]
    CS[...] = jnp.concatenate([tu0, fill], axis=0).T[C - 8 : C, :]

    turn = lax.rem(seams[0] + 1, C)
    fold_peers = (lax.rem(tile + n_lon - lon, n_lon), lax.rem(tile + 2 * n_lon - 1 - lon, n_lon))

    @pl.when(jnp.logical_not(has_north))
    def _():
        index = (turn + (2 * C - 1) - lane) & (C - 1)
        tu31 = wus[R - 1 : R, :] * peu[3] * um31
        for i, plane in enumerate((um31, um30, vm31, vm30, tu31, tv31)):
            SF[i] = -jnp.take_along_axis(plane, index, axis=1)

    @pl.when(has_north & has_south)
    def _():
        pl.semaphore_wait(barrier, 6)

    @pl.when(jnp.logical_not(has_south))
    def _():
        pl.semaphore_wait(barrier, 4)

    @pl.when(jnp.logical_not(has_north))
    def _():
        pl.semaphore_wait(barrier, n_lon + 1)

    def send(src, dst, i, a, b):
        return pltpu.make_async_remote_copy(
            src_ref=src, dst_ref=dst, send_sem=send_sem.at[i], recv_sem=recv_sem.at[i],
            device_id={"lat": a, "lon": b}, device_id_type=MESH,
        )

    def send_columns(src, dst, c, i, b):
        return pltpu.make_async_remote_copy(
            src_ref=src, dst_ref=dst, send_sem=lon_send.at[c, i], recv_sem=lon_recv.at[c, i],
            device_id={"lat": lat, "lon": b}, device_id_type=MESH,
        )

    to_north = send(SN, RS, 0, lat + 1, lon)
    to_south = send(SS, RN, 1, lat - 1, lon)
    to_northwest = send(CN, RCS, 2, lat + 1, west)
    to_southeast = send(CS, RCN, 3, lat - 1, east)
    to_east = [send_columns(TO.at[c, 0:5], RW.at[c], c, 0, east) for c in range(chunks)]
    to_west = [send_columns(TO.at[c, 5:11], RE.at[c], c, 1, west) for c in range(chunks)]

    def fold_copy(slot):
        return pltpu.make_async_remote_copy(
            src_ref=SF, dst_ref=G.at[slot], send_sem=fold_send.at[slot], recv_sem=fold_recv.at[slot],
            device_id={"lat": lat, "lon": fold_peers[slot]}, device_id_type=MESH,
        )

    def each_fold(act, own=None):
        for slot in range(2):
            mine = fold_peers[slot] == lon

            @pl.when(jnp.logical_not(has_north | mine))
            def _(slot=slot):
                act(slot)

            if own is not None:

                @pl.when(jnp.logical_not(has_north) & mine)
                def _(slot=slot):
                    own(slot)

    each_fold(lambda slot: fold_copy(slot).start())

    @pl.when(has_north)
    def _():
        to_north.start()
        to_northwest.start()

    @pl.when(has_south)
    def _():
        to_south.start()
        to_southeast.start()

    wide_u = jnp.concatenate([wus[...]] * 4, axis=0)
    wide_v = jnp.concatenate([wvs[...]] * 4, axis=0)

    def level_rows(k, o=0):
        return pl.ds(pl.multiple_of(k * pitch + 8, 8) + o, R)

    def columns(b, o, n=C):
        return pl.ds(pl.multiple_of(b * TP + 8, 8) + o, n)

    def pack(c, g):
        first = c * LC + 4 * g
        b = c * GB + g

        def whole(ref):
            return ref[pl.ds(first, 4)].reshape(4 * R, C)

        um = whole(mus).astype(f32) * whole(us)
        vm = whole(mvs).astype(f32) * whole(vs)
        tu = wide_u * whole(eus) * um
        tv = wide_v * whole(evs) * vm
        for i in range(4):
            part = slice(i * R, (i + 1) * R)
            to = level_rows(first + i)
            UM[to, :] = um[part]
            VM[to, :] = vm[part]
            TU[to, :] = tu[part]
            TV[to, :] = tv[part]
        turned = {"U": um.T, "V": vm.T, "T": tu.T, "S": tv.T}
        for name, ref in (("U", UT), ("V", VT), ("T", TT), ("S", ST)):
            ref[columns(b, 0), :] = turned[name]
        for row, (name, column) in enumerate(EAST + WEST):
            TO[c, row, pl.ds(g, 1), :] = turned[name][column : column + 1, :]

    per = 3 if GB % 3 == 0 else 2
    for c in range(chunks):
        for copy in full_copies[c]:
            copy.wait()

        def some(h, carry, c=c):
            for i in range(per):
                pack(c, h * per + i)
            return carry

        lax.fori_loop(0, GB // per, some, 0)
        to_east[c].start()
        to_west[c].start()

    sub = lax.broadcasted_iota(jnp.int32, (8, C), 0)
    lane_c = lax.broadcasted_iota(jnp.int32, (GB, C), 1)
    row_c = lax.broadcasted_iota(jnp.int32, (GB, C), 0)

    def stacked(parts):
        out = jnp.zeros((8, C), f32)
        for r, row in parts:
            out = jnp.where(sub == r, jnp.broadcast_to(row, (8, C)), out)
        return out

    def row_of(r):
        return pl.ds(8 + r, L, stride=pitch)

    def alone(b, carry):
        for i in range(4):
            k = 4 * b + i

            def get(ref, o):
                return ref[level_rows(k, o), :]

            um2, um1, u0, up1, up2 = (get(UM, o) for o in (-2, -1, 0, 1, 2))
            vm2, vm1, v0, vp1, vp2 = (get(VM, o) for o in (-2, -1, 0, 1, 2))
            sm, s0, sp = get(TV, -1), get(TV, 0), get(TV, 1)
            at = level_rows(k)
            QA[at, :] = q(um1, u0, up1, up2)
            QB[at, :] = q(um2, um1, u0, up1)
            DV[at, :] = (s0 + sp) * q(vm1, v0, vp1, vp2) - (sm + s0) * q(vm2, vm1, v0, vp1)
            CU[k] = mus[k].astype(f32) * FACTOR / (wus[...] * eus[k])
            CV[k] = mvs[k].astype(f32) * FACTOR / (wvs[...] * evs[k])
        return carry

    lax.fori_loop(0, L // 4, alone, 0)

    def across(ref, b, o, n=C):
        return ref[columns(b, o, n), :]

    def flux_u(b, o, n):
        return (across(TT, b, o - 1, n) + across(TT, b, o, n)) * q(*(across(UT, b, o + a, n) for a in (-2, -1, 0, 1)))

    def flux_v(b, o, n):
        return across(XT, b, o, n) * q(*(across(VT, b, o + a, n) for a in (-1, 0, 1, 2)))

    def inner_u(b, carry):
        FX[...] = flux_u(b, 0, C + 8)
        UT2[pl.ds(pl.multiple_of(b * C, 8), C), :] = FX[1 : C + 1, :] - FX[0:C, :]
        return carry

    lax.fori_loop(0, L // 4, inner_u, 0)

    @pl.when(has_south)
    def _():
        to_north.wait_recv()
        to_northwest.wait_recv()
        last = stacked(((0, RCS[0:1, :]),))
        KS[...] = jnp.concatenate([last, jnp.zeros((C - 8, C), f32)], axis=0).T[0:L, :]

    @pl.when(jnp.logical_not(has_south))
    def _():
        RS[...] = jnp.zeros_like(RS)
        KS[...] = jnp.zeros_like(KS)

    @pl.when(has_north)
    def _():
        to_south.wait_recv()
        to_southeast.wait_recv()
        KN[...] = RCN[7:8, :]

    def own_fold(slot):
        G[slot] = SF[...]

    each_fold(lambda slot: fold_copy(slot).wait_recv(), own_fold)

    @pl.when(jnp.logical_not(has_north))
    def _():
        for i in range(6):
            RN[i] = jnp.where(lane < turn, G[0, i], G[1, i])
        KN[...] = jnp.concatenate([G[0, 4], fill], axis=0).T[C - 1 : C, :]

    TU[row_of(R), :] = RN[4]
    below = RS[4]
    TS[row_of(-1), :] = below + roll(jnp.where(lane == 0, KS[...], below), -1)

    def edge_rows(c, carry):
        part = pl.ds(pl.multiple_of(c * LC, 8), LC)

        def at(r):
            return pl.ds(c * LC * pitch + 8 + r, LC, stride=pitch)

        def own(ref, first, n):
            return [ref[at(first + r), :] for r in range(n)]

        x = [RS[0, part, :], RS[1, part, :]] + own(UM, 0, 3)
        QB[at(0), :] = q(*x[0:4])
        middle = q(*x[1:5])
        QA[at(0), :] = middle
        QB[at(1), :] = middle
        x = own(UM, R - 3, 3) + [RN[0, part, :], RN[1, part, :]]
        middle = q(*x[0:4])
        QA[at(R - 2), :] = middle
        QB[at(R - 1), :] = middle
        QA[at(R - 1), :] = q(*x[1:5])
        for r, y, t in (
            (0, [RS[2, part, :], RS[3, part, :]] + own(VM, 0, 4), [RS[4, part, :]] + own(TV, 0, 3)),
            (R - 2, own(VM, R - 4, 4) + [RN[2, part, :], RN[3, part, :]], own(TV, R - 3, 3) + [RN[5, part, :]]),
        ):
            E = [(t[a] + t[a + 1]) * q(*y[a : a + 4]) for a in range(3)]
            DV[at(r), :] = E[1] - E[0]
            DV[at(r + 1), :] = E[2] - E[1]
        return carry

    lax.fori_loop(0, chunks, edge_rows, 0)

    def inner_v(h, carry):
        for i in range(per):
            b = h * per + i
            ts = [TU[level_rows(4 * b + j), :] + TU[level_rows(4 * b + j, 1), :] for j in range(4)]
            XT[columns(b, 0), :] = jnp.concatenate(ts, axis=0).T
        for i in range(per):
            b = h * per + i
            GX[...] = flux_v(b, -1, C + 8)
            VT2[pl.ds(pl.multiple_of(b * C, 8), C), :] = GX[1 : C + 1, :] - GX[0:C, :]
        return carry

    lax.fori_loop(0, chunks * GB // per, inner_v, 0)

    spread = lax.broadcasted_iota(jnp.int32, (C, C), 0) % 4 * R + (R - 1)
    spread = jnp.where(spread == lax.broadcasted_iota(jnp.int32, (C, C), 1), 1.0, 0.0).astype(f32)
    for c in range(chunks):
        to_east[c].wait_recv()
        to_west[c].wait_recv()
        corner = jnp.where(lane_c // 4 == row_c + c * GB, jnp.broadcast_to(KN[...], (GB, C)), 0.0)
        corner = lax.dot_general(
            corner, spread, (((1,), (0,)), ((), ())),
            precision=lax.Precision.HIGHEST, preferred_element_type=f32,
        )
        tw = RW[c, 4]
        xw = tw + jnp.where(lane_c % R == R - 1, corner, roll(tw, -1))
        for g in range(GB):
            b = c * GB + g
            row = slice(g, g + 1)
            for ref, o, value in (
                (UT, -2, RW[c, 0, row]), (UT, -1, RW[c, 1, row]),
                (VT, -2, RW[c, 2, row]), (VT, -1, RW[c, 3, row]),
                (TT, -1, RW[c, 4, row]), (XT, -1, xw[row]),
                (UT, C, RE[c, 0, row]), (UT, C + 1, RE[c, 1, row]),
                (VT, C, RE[c, 2, row]), (VT, C + 1, RE[c, 3, row]),
                (TT, C, RE[c, 4, row]), (ST, C, RE[c, 5, row]),
            ):
                ref[b * TP + 8 + o : b * TP + 9 + o, :] = value

    def finish(b):
        def outer(flux, ref, shift):
            at = pl.multiple_of(b * C, 8)
            low = flux(b, shift + 1, 8) - flux(b, shift, 8)
            high = flux(b, C - 7 + shift, 8) - flux(b, C - 8 + shift, 8)
            return jnp.concatenate([low, ref[pl.ds(at + 8, C - 16), :], high], axis=0).T

        du = outer(flux_u, UT2, 0)
        dv = outer(flux_v, VT2, -1)
        ts = (across(ST, b, 0) + across(ST, b, 1)).T
        for i in range(4):
            k = 4 * b + i
            part = slice(i * R, (i + 1) * R)
            at = level_rows(k)
            TS[at, :] = ts[part]
            step = du[part] + ts[part] * QA[at, :] - TS[level_rows(k, -1), :] * QB[at, :]
            ou[k] = UM[at, :] - CU[k] * step
            ov[k] = VM[at, :] - CV[k] * (dv[part] + DV[at, :])

    def some_blocks(h, carry):
        for i in range(per):
            finish(h * per + i)
        return carry

    lax.fori_loop(0, chunks * GB // per, some_blocks, 0)

    for c in range(chunks):
        to_east[c].wait_send()
        to_west[c].wait_send()

    @pl.when(has_north)
    def _():
        to_north.wait_send()
        to_northwest.wait_send()

    @pl.when(has_south)
    def _():
        to_south.wait_send()
        to_southeast.wait_send()

    each_fold(lambda slot: fold_copy(slot).wait_send())


PIECES = 4


def write_out(L, nu, nv, ou, ov, sem):
    n = L // PIECES
    copies = [
        pltpu.make_async_copy(src.at[pl.ds(p * n, n)], dst.at[pl.ds(p * n, n)], sem.at[i, p])
        for p in range(PIECES)
        for i, (src, dst) in enumerate(((nu, ou), (nv, ov)))
    ]
    for copy in copies:
        copy.start()
    for copy in copies:
        copy.wait()


def local(n_lat, n_lon, u, v, eu, ev, wu, wv, mu, mv, seam):
    L, R, C = u.shape
    cube = (L, R, C)
    LC = 24 if L % 24 == 0 else 8
    chunks, GB = L // LC, LC // 4
    vm = pltpu.VMEM
    dma = pltpu.SemaphoreType.DMA
    scratch = (
        [vm(cube, f32)] * 4
        + [vm((R, C), f32)] * 2
        + [vm(cube, jnp.int32)] * 2
        + [pltpu.SMEM(seam.shape, jnp.int32)]
        + [vm((4, L, C), f32)] * 2
        + [vm((4, L, C), jnp.int32)] * 2
        + [vm((4, L, C), f32)] * 2
        + [vm((L * (R + 8) + 16, C), f32)] * 8
        + [vm(cube, f32)] * 2
        + [vm((chunks * GB * TP + 8, C), f32)] * 5
        + [vm((chunks * GB * C, C), f32)] * 2
        + [vm((C + 8, C), f32)] * 2
        + [vm((5, L, C), f32), vm((6, L, C), f32), vm((6, L, C), f32)]
        + [vm((8, C), f32)] * 2
        + [vm((5, L, C), f32), vm((6, L, C), f32)]
        + [vm((8, C), f32)] * 2
        + [vm((2, 6, L, C), f32)]
        + [vm((L, C), f32), vm((1, C), f32)]
        + [vm((chunks, 11, GB, C), f32)]
        + [vm((chunks, 5, GB, C), f32), vm((chunks, 6, GB, C), f32)]
        + [dma((chunks, 6)), dma((27,)), dma((4,)), dma((4,)), dma((2,)), dma((2,)), dma((chunks, 2)), dma((chunks, 2))]
    )
    hbm = pl.BlockSpec(memory_space=pltpu.HBM)

    def step(tile, *operands):
        return pl.pallas_call(
            functools.partial(kernel, n_lat, n_lon, L, R, C, LC, tile),
            out_shape=[jax.ShapeDtypeStruct(cube, f32)] * 2,
            in_specs=[hbm] * 9,
            out_specs=[pl.BlockSpec(memory_space=pltpu.VMEM)] * 2,
            scratch_shapes=scratch,
            compiler_params=pltpu.CompilerParams(
                collective_id=tile, has_side_effects=True, vmem_limit_bytes=44 * 1024 * 1024
            ),
        )(*(pltpu.with_memory_space_constraint(x, pltpu.HBM) for x in operands))

    tile = lax.rem((seam[0] + 1) // C, n_lon)
    branches = [functools.partial(step, t) for t in range(n_lon)]
    nu, nv = lax.switch(tile, branches, u, v, eu, ev, wu, wv, mu, mv, seam)
    return tuple(
        pl.pallas_call(
            functools.partial(write_out, L),
            out_shape=[jax.ShapeDtypeStruct(cube, f32)] * 2,
            in_specs=[pl.BlockSpec(memory_space=pltpu.VMEM)] * 2,
            out_specs=[hbm] * 2,
            scratch_shapes=[dma((2, PIECES))],
            compiler_params=pltpu.CompilerParams(vmem_limit_bytes=1024 * 1024),
        )(*(pltpu.with_memory_space_constraint(x, pltpu.VMEM) for x in (nu, nv)))
    )


def solution(mesh):
    n_lat, n_lon = mesh.shape["lat"], mesh.shape["lon"]
    cube = P(None, "lat", "lon")
    flat = P("lat", "lon")
    return jax.shard_map(
        functools.partial(local, n_lat, n_lon),
        mesh=mesh,
        in_specs=(cube, cube, cube, cube, flat, flat, cube, cube, P()),
        out_specs=(cube, cube),
        check_vma=False,
    )
```

time: 25.7 us -> 24.7 us (0.961)
  the two profiles are of different devices: /device:TPU:105 before, /device:TPU:225 now
where the time goes in v4:
time: 24.7 us; the launch traced here: 24.4 us
  Pallas kernels  21.5 us (87%)
  between operations  1.5 us (6%)
  local copies, waits for them, and re-layouts  1.2 us (5%)
  loops' own time  0.26 us (1%)
    pallas_call x1, Pallas kernels, step(): pl.pallas_call(functools.partial(kernel, n_lat, n_lon, L, R, C, LC, tile)...  20 us
    pallas_call x1, Pallas kernels, local(): pl.pallas_call(functools.partial(write_out, L), out_shape=[jax.ShapeDtype...  1.47 us
    slice x1, local copies, waits for them, and re-layouts, local(): tile = lax.rem((seam[0] + 1) // C, n_lon)  1.2 us

profile of v4, /device:TPU:225, one launch (start us, length us, event | category | flops | bytes accessed | tf_op | source)
XLA Modules:
  0.0 24.4 jit_solution(17869837835671653300)
XLA Ops:
  0.6 1.2 %slice.3 = s32[1]{0:T(128)} slice(s32[1024]{0:T(1024)} %param.25), slice={[0:1]} | slice | bytes 8 | tf_op jit(solution)/shard_map/slice | solution.py:497
  2.5 20.3 %conditional.1 = ((f32[72,32,128]{2,1,0:T(8,128)S(1)}, f32[72,32,128]{2,1,0:T(8,128)S(1)})) conditional(s32[]{:T(128)} %clamp.3, (f32[72,32,128]{2,1,0:T(8,128)}, f32[72,32,128]{2,1,0:T(8,128)}, f32[72,32,128]{2,1,0:T(8,128)}, f32[72,32,128]{2,1,0:T(8,128)}, f32[32,128]{1,0:T(8,128)}, /*index=5*/f32[32,128]{1,0:T(8,128)}, ...), branch_computations={%region_0.1_spmd, %region_1.2_spmd, %region_2.3_spmd, %region_3.4_... | conditional | bytes 8 | solution.py:499
  2.5 20.0 %branch_3_fun.1 = (f32[72,32,128]{2,1,0:T(8,128)S(1)}, f32[72,32,128]{2,1,0:T(8,128)S(1)}) custom-call(f32[72,32,128]{2,1,0:T(8,128)} %get-tuple-element.171.u, f32[72,32,128]{2,1,0:T(8,128)} %get-tuple-element.172.v, f32[72,32,128]{2,1,0:T(8,128)} %get-tuple-element.173.eu, f32[72,32,128]{2,1,0:T(8,128)} %get-tuple-element.174.ev, ...), custom_call_target="tpu_custom_call" | custom-call | tf_op jit(solution)/shard_map/cond/branch_3_fun/pallas_call | solution.py:486
  22.8 1.5 %shard_map.104 = (f32[72,32,128]{2,1,0:T(8,128)}, f32[72,32,128]{2,1,0:T(8,128)}) custom-call(f32[72,32,128]{2,1,0:T(8,128)S(1)} %get-tuple-element.220.nu, f32[72,32,128]{2,1,0:T(8,128)S(1)} %get-tuple-element.221.nv), custom_call_target="tpu_custom_call" | custom-call | tf_op jit(solution)/shard_map/pallas_call | solution.py:501
